TPU v7x, 32 devices: a whole 2x2x4 slice. The times are simulated.
32 devices in a mesh: ga: 8 (over z, y), band: 4 (over x, core).
Axes of the slice: x: 2, y: 2, z: 4, core: 2. Of those that a mesh axis runs over, the one named last changes fastest.
Arguments:
- coeffs: bfloat16 [2048, 128], P('ga', 'band'), may hold values from -6 to 6
- coupling: bfloat16 [12288, 12288], P('ga', 'band'), may hold values from -0.21875 to 0.21875
- miller: int32 [3, 2048], P(None, 'ga'), may hold values from -24 to 24
- species: int32 [1024], replicated, may hold values from 0 to 3
- proj_atom: int32 [12288], replicated, may hold values from 0 to 1023, as said below
- positions: float32 [3, 1024], replicated, may hold values from 0 to 1
- radial: float32 [12, 128], replicated, may hold values from -8 to 8
Outputs:
- result: bfloat16 [2048, 128], P('ga', 'band')
Inputs may be any that keep to these rules, and one draw needn't show every extreme that they name: `proj_atom`: projector p has channel p mod 12; each atom owns 12 consecutive projectors.
All inputs are finite; a program needn't handle non-finite values.
Results may differ from a plain program's by a relative error of at most 0.008.
Values may be sent and summed in bfloat16 or wider, within the bound.
No kernel may reach another device: no remote copies, remote signals or barrier semaphores. Data moves between devices by JAX's collectives and lax.ppermute only.
A program may use at most 128 MiB of HBM per device.

v0:
```python
import math

import jax
import jax.numpy as jnp
from jax import lax
from jax.sharding import PartitionSpec as P

NCH = 12
SHELLS = 3
KINDS = 4
QBINS = 128
MMAX = 24
NPROJ = 12288


def radial_values(miller_block, radial):
    mf = miller_block.astype(jnp.float32)
    qval = (mf[0] * mf[0] + mf[1] * mf[1] + mf[2] * mf[2]) * ((QBINS - 1) / (3.0 * MMAX * MMAX))
    knots = jnp.arange(QBINS, dtype=jnp.int32).astype(jnp.float32)
    hats = jnp.maximum(0.0, 1.0 - jnp.abs(qval[:, None] - knots[None, :]))
    return jnp.dot(hats, radial.T, precision=lax.Precision.HIGHEST)


def beta_columns(miller_block, radval, species, proj_atom, positions, start, count, scale):
    mf = miller_block.astype(jnp.float32)
    atoms = lax.dynamic_slice_in_dim(proj_atom, jnp.asarray(start).astype(jnp.int32), count)
    channel = (jnp.asarray(start).astype(jnp.int32) + jnp.arange(count, dtype=jnp.int32)) % NCH
    shell = channel // 4
    comp = channel % 4
    kind = jnp.take(species, atoms)
    column = kind * SHELLS + shell
    select = (column[None, :] == jnp.arange(KINDS * SHELLS, dtype=jnp.int32)[:, None]).astype(
        jnp.float32
    )
    radpart = jnp.dot(radval, select, precision=lax.Precision.HIGHEST)
    place = jnp.take(positions, atoms, axis=1)
    theta = (
        2.0
        * math.pi
        * (
            mf[0][:, None] * place[0][None, :]
            + mf[1][:, None] * place[1][None, :]
            + mf[2][:, None] * place[2][None, :]
        )
    )
    unit = mf / MMAX
    angular = jnp.where(
        comp[None, :] == 1,
        unit[0][:, None],
        jnp.where(
            comp[None, :] == 2,
            unit[1][:, None],
            jnp.where(comp[None, :] == 3, unit[2][:, None], jnp.ones_like(theta)),
        ),
    )
    phase = jnp.where(comp[None, :] == 0, jnp.cos(theta), jnp.sin(theta))
    return (radpart * angular * phase * scale).astype(jnp.bfloat16)


def beta_atoms(miller_block, radval, species, proj_atom, positions, start, count, scale):
    mf = miller_block.astype(jnp.float32)
    npw = mf.shape[1]
    natoms = count // NCH
    owners = lax.dynamic_slice_in_dim(proj_atom, jnp.asarray(start).astype(jnp.int32), count)
    atoms = owners.reshape(natoms, NCH)[:, 0]
    kind = jnp.take(species, atoms)
    column = kind[:, None] * SHELLS + jnp.arange(SHELLS, dtype=jnp.int32)[None, :]
    select = (
        column.reshape(-1)[None, :] == jnp.arange(KINDS * SHELLS, dtype=jnp.int32)[:, None]
    ).astype(jnp.float32)
    radpart = jnp.dot(radval, select, precision=lax.Precision.HIGHEST).reshape(npw, natoms, SHELLS)
    place = jnp.take(positions, atoms, axis=1)
    theta = (
        2.0
        * math.pi
        * (
            mf[0][:, None] * place[0][None, :]
            + mf[1][:, None] * place[1][None, :]
            + mf[2][:, None] * place[2][None, :]
        )
    )
    cosine = jnp.cos(theta)
    sine = jnp.sin(theta)
    unit = mf / MMAX
    ones = jnp.ones((npw, natoms), jnp.float32)
    angular = jnp.stack(
        [
            ones,
            jnp.broadcast_to(unit[0][:, None], (npw, natoms)),
            jnp.broadcast_to(unit[1][:, None], (npw, natoms)),
            jnp.broadcast_to(unit[2][:, None], (npw, natoms)),
        ],
        axis=2,
    )
    phase = jnp.stack([cosine, sine, sine, sine], axis=2)
    values = radpart[:, :, :, None] * angular[:, :, None, :] * phase[:, :, None, :] * scale
    return values.reshape(npw, count).astype(jnp.bfloat16)


def make_beta(miller_block, radval, species, proj_atom, positions, start, count, scale, aligned):
    if aligned and count % NCH == 0:
        return beta_atoms(miller_block, radval, species, proj_atom, positions, start, count, scale)
    return beta_columns(miller_block, radval, species, proj_atom, positions, start, count, scale)


def block_size(count):
    width = 1
    for cand in range(min(count, 768), 0, -1):
        if count % cand == 0:
            width = cand
            break
    return width


def shards(coeffs, coupling, miller, species, proj_atom, positions, radial):
    scale = 1.0 / math.sqrt(coeffs.shape[0] * lax.axis_size("ga"))
    radval = radial_values(miller, radial)
    nbands = coeffs.shape[1]
    aligned = coupling.shape[0] % NCH == 0
    width = block_size(NPROJ)
    starts = width * jnp.arange(NPROJ // width, dtype=jnp.int32)

    def one_block(first):
        beta = make_beta(
            miller, radval, species, proj_atom, positions, first, width, scale, aligned
        )
        return lax.dot_general(
            beta, coeffs, (((0,), (0,)), ((), ())), preferred_element_type=jnp.float32
        )

    summed = lax.psum(lax.map(one_block, starts).reshape(NPROJ, nbands), "ga")
    proj_b = summed.astype(jnp.bfloat16)
    full_rows = lax.all_gather(coupling, "band", axis=1, tiled=True)
    mixed = jnp.dot(full_rows, proj_b, preferred_element_type=jnp.float32).astype(jnp.bfloat16)
    piece = jax.tree.map(lambda part: lax.all_gather(part, "ga", axis=0, tiled=True), mixed)
    start = jnp.int32(0)
    count = piece.shape[0]
    add_width = block_size(count)

    def step(index, acc):
        first = start + index * add_width
        beta = make_beta(
            miller, radval, species, proj_atom, positions, first, add_width, scale, aligned
        )
        rows = lax.dynamic_slice_in_dim(piece, index * add_width, add_width, 0)
        return acc + jnp.dot(beta, rows, preferred_element_type=jnp.float32)

    summed_back = lax.fori_loop(0, count // add_width, step, coeffs.astype(jnp.float32))
    return summed_back.astype(jnp.bfloat16)


def solution(mesh):
    placed = (P("ga", "band"), P("ga", "band"), P(None, "ga"), P(), P(), P(), P())
    return jax.shard_map(
        shards, mesh=mesh, in_specs=placed, out_specs=P("ga", "band"), check_vma=False
    )
```

profile of v0, /device:TPU:0, one launch (start us, length us, event | category | flops | bytes accessed | tf_op | source)
XLA Modules:
  0.0 415.5 jit_solution(7675885683890201779)
XLA Ops:
  7.9 172.2 %while.27 = (s32[]{:T(128)}, f32[16,768,32]{1,0,2:T(8,128)S(1)}, s32[16]{0:T(128)S(1)}, s32[12288]{0:T(1024)}, s32[1024]{0:T(1024)S(1)}, /*index=5*/f32[256,12]{...) while((s32[]{:T(128)}, f32[16,768,32]{1,0,2:T(8,128)S(1)}, ...), condition=%wide.region_1.4_spmd, body=%wide.region_0.3_spmd.sunk | while | flops 20943940 | bytes 5160803 | solution.py:131
  15.5 3.2 dynamic_update_slice.7
  21.2 0.8 dynamic_slice.36
  26.3 3.2 dynamic_update_slice.7
  32.0 0.8 dynamic_slice.36
  37.1 3.2 dynamic_update_slice.7
  42.8 0.8 dynamic_slice.36
  47.8 3.2 dynamic_update_slice.7
  53.5 0.8 dynamic_slice.36
  58.6 3.2 dynamic_update_slice.7
  69.3 3.2 dynamic_update_slice.7
  80.1 3.2 dynamic_update_slice.7
  85.8 0.8 dynamic_slice.36
  90.9 3.2 dynamic_update_slice.7
  96.6 0.8 dynamic_slice.36
  101.6 3.2 dynamic_update_slice.7
  107.3 0.8 dynamic_slice.36
  112.4 3.2 dynamic_update_slice.7
  118.1 0.8 dynamic_slice.36
  123.2 3.2 dynamic_update_slice.7
  128.9 0.8 dynamic_slice.36
  133.9 3.2 dynamic_update_slice.7
  139.6 0.8 dynamic_slice.36
  144.7 3.2 dynamic_update_slice.7
  155.5 3.2 dynamic_update_slice.7
  161.2 0.8 dynamic_slice.36
  166.2 3.2 dynamic_update_slice.7
  177.0 3.2 dynamic_update_slice.7
  180.2 0.8 copy-done.2
  181.0 0.9 copy.30
  181.9 82.5 %all-reduce.1 = bf16[12288,32]{0,1:T(8,128)(2,1)S(1)} all-reduce(f32[12288,32]{0,1:T(8,128)S(1)} %bitcast.98), channel_id=1, replica_groups=mesh['ga'=8,'band'=4] {'ga'}, use_global_device_ids=true, to_apply=%region_2.0 | all-reduce | flops 393216 | bytes 2359296 | tf_op jit(solution)/shard_map/psum | solution.py:131
  264.5 16.8 %fusion.8 = bf16[1536,32]{0,1:T(8,128)(2,1)S(1)} fusion(bf16[1536,12288]{1,0:T(8,128)(2,1)} %all-gather.2.cloned.1.call-done, bf16[12288,32]{0,1:T(8,128)(2,1)S(1)} %all-reduce.1), kind=kOutput, calls=%fused_computation.49 | convolution fusion | flops 1208008704 | bytes 38633472 | tf_op jit(solution)/shard_map/dot_general | solution.py:134
  281.3 32.0 %all_gather.7 = bf16[12288,32]{0,1:T(8,128)(2,1)S(1)} all-gather(bf16[1536,32]{0,1:T(8,128)(2,1)S(1)} %fusion.8), channel_id=1, replica_groups=mesh['ga'=8,'band'=4] {'ga'}, dimensions={0}, use_global_device_ids=true | all-gather | bytes 884736 | tf_op jit(solution)/shard_map/all_gather | solution.py:135
  313.2 94.7 %while.28 = (s32[]{:T(128)}, f32[256,32]{0,1:T(8,128)S(1)}, s32[12288]{0:T(1024)}, s32[1024]{0:T(1024)S(1)}, f32[256,12]{0,1:T(8,128)S(1)}, /*index=5*/f32[3,256...) while((s32[]{:T(128)}, f32[256,32]{0,1:T(8,128)S(1)}, ...), condition=%wide.region_4.7_spmd, body=%wide.region_3.6_spmd.sunk | while | flops 20952132 | bytes 4767587 | solution.py:148
  315.0 1.6 gather_fusion.2
  319.2 0.8 dynamic_slice.38
  320.9 1.6 gather_fusion.2
  325.1 0.8 dynamic_slice.38
  326.8 1.6 gather_fusion.2
  331.0 0.8 dynamic_slice.38
  332.8 1.6 gather_fusion.2
  336.9 0.8 dynamic_slice.38
  338.7 1.6 gather_fusion.2
  342.8 0.8 dynamic_slice.38
  344.6 1.6 gather_fusion.2
  348.8 0.8 dynamic_slice.38
  350.5 1.6 gather_fusion.2
  354.7 0.8 dynamic_slice.38
  356.5 1.6 gather_fusion.2
  360.6 0.8 dynamic_slice.38
  362.4 1.6 gather_fusion.2
  366.5 0.8 dynamic_slice.38
  368.3 1.6 gather_fusion.2
  372.5 0.8 dynamic_slice.38
  374.2 1.6 gather_fusion.2
  378.4 0.8 dynamic_slice.38
  380.1 1.6 gather_fusion.2
  384.3 0.8 dynamic_slice.38
  386.1 1.6 gather_fusion.2
  390.2 0.8 dynamic_slice.38
  392.0 1.6 gather_fusion.2
  396.1 0.8 dynamic_slice.38
  397.9 1.6 gather_fusion.2
  403.8 1.6 gather_fusion.2
  (910 shorter events, 136.4 us)
Async XLA Ops:
  6.5 1.1 copy-start
  6.5 0.8 copy-start.5
  6.5 0.8 copy-start.4
  6.5 1.0 copy-start.3
  6.5 1.4 copy-start.1
  6.5 257.9 %all-gather.2.cloned.1.call-start = ((), (), s32[]{:S(2)}) async-start(), calls=%async_computation | async-start | bytes 47185920 | tf_op jit(solution)/shard_map/all_gather | solution.py:133
  180.2 0.8 copy-start.2
Sparse Core Ops, SparseCore 0:
  8.9 229.8 all-gather.1
where the time goes:
time: 418 us; the launch traced here: 415 us
  local copies, waits for them, and re-layouts  181 us (43%)
  blocking collectives  114 us (27%)
  other arithmetic  37.1 us (9%)
  loops' own time  35.3 us (8%)
  matrix products  33.3 us (8%)
  between operations  13.6 us (3%)
    psum x1, blocking collectives, shards(): summed = lax.psum(lax.map(one_block, starts).reshape(NPROJ, nbands), 'ga')  82.5 us
    dynamic_update_slice x32, local copies, waits for them, and re-layouts, shards(): summed = lax.psum(lax.map(one_block, starts).reshape(NPROJ, nbands), 'ga')  53.2 us
    gather x32, local copies, waits for them, and re-layouts, beta_atoms(): place = jnp.take(positions, atoms, axis=1)  35.9 us
    another operation x1, loops' own time, shards(): summed = lax.psum(lax.map(one_block, starts).reshape(NPROJ, nbands), 'ga')  32.7 us
    all_gather x1, blocking collectives, shards(): lax.all_gather(part, 'ga', axis=0, tiled=True)  32 us
    dynamic_slice x32, local copies, waits for them, and re-layouts, beta_atoms(): lax.dynamic_slice_in_dim(proj_atom, jnp.asarray(start).astype(jnp.int32),...  25 us
    gather x32, local copies, waits for them, and re-layouts, beta_atoms(): kind = jnp.take(species, atoms)  23.3 us
    dot_general x1, matrix products, shards(): jnp.dot(full_rows, proj_b, preferred_element_type=jnp.float32)  16.8 us
  transfers between devices with their start and end apart: 1, of which 0 were waited for; matrix products, arithmetic and copies ran while one was open for 34% of the time, Pallas kernels for 0%

commit v1 on v0

v1 whole, which is shorter than its diff:
```python
import functools
import math

import jax
import jax.numpy as jnp
from jax import lax
from jax.experimental import pallas as pl
from jax.experimental.pallas import tpu as pltpu
from jax.sharding import PartitionSpec as P

NCH = 12
SHELLS = 3
COMPS = 4
MMAX = 24
LANES = 128
SPLITS = 3

SIN_POLY = (4.442882919124345, -7.308245686509103, 3.6063542184332804, -0.8461116503752865, 0.10982451642699691)
COS_POLY = (1.4142134962552289, -6.978850948563853, 5.7394603769076955, -1.8835579059892091, 0.31068802753070307)


def horner(coefs, z):
    acc = jnp.float32(coefs[-1])
    for c in coefs[-2::-1]:
        acc = acc * z + jnp.float32(c)
    return acc


def cos_sin_turns(turns):
    r = turns - jnp.round(turns)
    z = r * r
    s = horner(SIN_POLY, z) * r
    c = horner(COS_POLY, z)
    return 1.0 - s * s, s * c


def split3(x):
    hi = x.astype(jnp.bfloat16)
    rest = x - hi.astype(jnp.float32)
    mid = rest.astype(jnp.bfloat16)
    lo = (rest - mid.astype(jnp.float32)).astype(jnp.bfloat16)
    return hi, mid, lo


def nt_dot(a, b):
    return lax.dot_general(a, b, (((1,), (1,)), ((), ())), preferred_element_type=jnp.float32)


def nn_dot(a, b):
    return jnp.dot(a, b, preferred_element_type=jnp.float32)


def pack_kernel(coef_ref, mil_ref, out_ref):
    half = coef_ref.shape[1] // 2
    npw = coef_ref.shape[0]
    ct = coef_ref[...].astype(jnp.float32).T
    m = mil_ref[...].astype(jnp.float32)
    ngroups = npw // LANES
    mrows = [m[c : c + 1, g * LANES : (g + 1) * LANES] for c in range(3) for g in range(ngroups)]
    used = len(mrows)
    pad = out_ref.shape[2] - half * ngroups - used
    if pad:
        mrows.append(jnp.zeros((pad, LANES), jnp.float32))
    for h in range(2):
        rows = [ct[h * half : (h + 1) * half, g * LANES : (g + 1) * LANES] for g in range(ngroups)]
        block = jnp.concatenate(rows + mrows, axis=0).astype(jnp.bfloat16)
        out_ref[:, h] = jnp.broadcast_to(block[None], (out_ref.shape[0],) + block.shape)


def pack(coeffs, miller, ndev):
    npw, nbl = coeffs.shape
    ngroups = npw // LANES
    rows = -(-(nbl // 2 * ngroups + 3 * ngroups) // 8) * 8
    out = pl.pallas_call(
        pack_kernel,
        out_shape=jax.ShapeDtypeStruct((ndev // 2, 2, rows, LANES), jnp.bfloat16),
        name="pack",
    )(coeffs, miller)
    return out.reshape(ndev, rows, LANES)


def table_kernel(atc_ref, atr_ref, sp_ref, pos_ref, xc_ref, xr_ref, oc_ref, or_ref, *, kinds):
    natoms = sp_ref.shape[1]
    width = oc_ref.shape[2]
    per = width // SPLITS
    hi, mid, lo = split3(pos_ref[...])
    sp = sp_ref[...]
    row = lax.broadcasted_iota(jnp.int32, (width, natoms), 0) % per
    for at_ref, x_ref, o_ref in ((atc_ref, xc_ref, oc_ref), (atr_ref, xr_ref, or_ref)):
        n = at_ref.shape[0]
        pick = (lax.broadcasted_iota(jnp.int32, (n, natoms), 1) == at_ref[...]).astype(jnp.bfloat16)
        x = nt_dot(pick, hi) + nt_dot(pick, mid) + nt_dot(pick, lo)
        for c in range(3):
            x_ref[c] = jnp.broadcast_to(x[:, c : c + 1], (n, LANES))
        for s in range(SHELLS):
            kind_rows = ((row - s * kinds) == sp).astype(jnp.bfloat16)
            o_ref[s] = nt_dot(pick, kind_rows).astype(jnp.bfloat16)


def main_kernel(
    ra_ref, rb_ref, xc_ref, xr_ref, oc_ref, or_ref, rad_ref, b_hbm, own_ref, oth_ref,
    b_ref, sem, ms_ref, rads_ref, sel_ref, gc_ref, gs_ref, acc_ref, proj_ref, mix_ref,
    *, nband, scale, qscale, chunk,
):
    nga = ms_ref.shape[0]
    npw = ms_ref.shape[2]
    ngroups = npw // LANES
    half = own_ref.shape[1] // nband
    nb = 2 * own_ref.shape[1]
    nc = xc_ref.shape[1]
    nr = xr_ref.shape[1]
    nrows = b_ref.shape[0]
    qbins = rad_ref.shape[1]
    per = rads_ref.shape[1] // SPLITS

    copies = [
        pltpu.make_async_copy(b_hbm.at[pl.ds(k * chunk, chunk)], b_ref.at[pl.ds(k * chunk, chunk)], sem.at[k])
        for k in range(nrows // chunk)
    ]
    for copy in copies:
        copy.start()

    def prepare(i, carry):
        raw = ra_ref[i * nband, half * ngroups :, :].astype(jnp.float32)
        comps = [
            jnp.concatenate([raw[c * ngroups + g : c * ngroups + g + 1] for g in range(ngroups)], axis=1)
            for c in range(3)
        ]
        m = jnp.concatenate(comps + [jnp.zeros((5, npw), jnp.float32)], axis=0)
        ms_ref[i] = m
        q = (comps[0] * comps[0] + comps[1] * comps[1] + comps[2] * comps[2]) * jnp.float32(qscale)
        knot = lax.broadcasted_iota(jnp.int32, (qbins, npw), 0).astype(jnp.float32)
        hats = jnp.maximum(0.0, 1.0 - jnp.abs(q - knot))
        hi = hats.astype(jnp.bfloat16)
        lo = (hats - hi.astype(jnp.float32)).astype(jnp.bfloat16)
        table = rad_ref[...]
        r = nn_dot(table, hi) + nn_dot(table, lo)
        r = (r[0:per] + r[per : 2 * per] + r[2 * per : 3 * per]) * jnp.float32(scale)
        rads_ref[i] = jnp.concatenate(split3(r), axis=0)
        return carry

    lax.fori_loop(0, nga, prepare, 0)

    def build(i, x_ref, o_ref, n):
        rads = rads_ref[i]
        for s in range(SHELLS):
            sel_ref[s, :n] = nn_dot(o_ref[s], rads)
        m = [ms_ref[i, c : c + 1, :] for c in range(3)]
        step = 16 if n % 16 == 0 else n
        for a in range(0, n, step):
            turns = 0.0
            for c in range(3):
                x = x_ref[c, a : a + step, :]
                turns = turns + jnp.concatenate([x] * ngroups, axis=1) * m[c]
            cos, sin = cos_sin_turns(turns)
            for s in range(SHELLS):
                sel = sel_ref[s, a : a + step, :]
                gc_ref[s * n + a : s * n + a + step, :] = (sel * cos).astype(jnp.bfloat16)
                gs_ref[s * n + a : s * n + a + step, :] = (sel * sin).astype(jnp.bfloat16)

    def weights(i):
        return [ms_ref[i, c : c + 1, :] * jnp.float32(1.0 / MMAX) for c in range(3)]

    def coefs(i):
        rows = []
        for ref in (ra_ref, rb_ref):
            for j in range(nband):
                rows.append(
                    jnp.concatenate(
                        [ref[i * nband + j, g * half : (g + 1) * half, :] for g in range(ngroups)], axis=1
                    )
                )
        return jnp.concatenate(rows, axis=0)

    acc_ref[...] = jnp.zeros(acc_ref.shape, jnp.float32)

    def project(i, carry):
        build(i, xc_ref, oc_ref, nc)
        c = coefs(i)
        cf = c.astype(jnp.float32)
        w = weights(i)
        wc = jnp.concatenate([(cf * w[k]).astype(jnp.bfloat16) for k in range(3)], axis=0)
        rows = SHELLS * nc
        acc_ref[:, :nb] += nt_dot(gc_ref[:rows, :], c)
        acc_ref[:, nb:] += nt_dot(gs_ref[:rows, :], wc)
        return carry

    lax.fori_loop(0, nga, project, 0)

    for s in range(SHELLS):
        for t in range(COMPS):
            proj_ref[pl.ds(COMPS * s + t, nc, stride=NCH), :] = acc_ref[
                s * nc : (s + 1) * nc, t * nb : (t + 1) * nb
            ]
    proj = proj_ref[...].astype(jnp.bfloat16)

    for k, copy in enumerate(copies):
        copy.wait()
        mix_ref[k * chunk : (k + 1) * chunk, :] = nn_dot(b_ref[k * chunk : (k + 1) * chunk, :], proj)

    mixed = []
    for t in range(COMPS):
        m = jnp.concatenate(
            [mix_ref[pl.ds(COMPS * s + t, nr, stride=NCH), :] for s in range(SHELLS)], axis=0
        )
        mixed.append(m.T)
    m0 = mixed[0].astype(jnp.bfloat16)
    mt = jnp.concatenate(mixed[1:], axis=0).astype(jnp.bfloat16)

    def expand(i, carry):
        build(i, xr_ref, or_ref, nr)
        rows = SHELLS * nr
        y = nn_dot(m0, gc_ref[:rows, :])
        ys = nn_dot(mt, gs_ref[:rows, :])
        w = weights(i)
        for k in range(3):
            y = y + w[k] * ys[k * nb : (k + 1) * nb]
        own_ref[i] = y[: nb // 2]
        oth_ref[i] = y[nb // 2 :].astype(jnp.bfloat16)
        return carry

    lax.fori_loop(0, nga, expand, 0)


def row_chunk(count):
    for cand in range(min(count, 512), 0, -1):
        if count % cand == 0 and cand % 8 == 0:
            return cand
    return count


def finish_kernel(recv_ref, coef_ref, out_ref):
    n = recv_ref.shape[0]
    parts = []
    for h in range(2):
        def add(k, acc, h=h):
            return acc + recv_ref[k, h].astype(jnp.float32)
        parts.append(lax.fori_loop(0, n, add, jnp.zeros(recv_ref.shape[2:], jnp.float32), unroll=8))
    total = jnp.concatenate(parts, axis=0).T
    out_ref[...] = (coef_ref[...].astype(jnp.float32) + total).astype(out_ref.dtype)


def shards(coeffs, coupling, miller, species, proj_atom, positions, radial):
    nga = lax.axis_size("ga")
    nband = lax.axis_size("band")
    ndev = nga * nband
    axes = ("ga", "band")
    npw, nbl = coeffs.shape
    half = nbl // 2
    nb = nbl * nband
    nrows, ncols = coupling.shape
    nr, nc = nrows // NCH, ncols // NCH
    kinds = radial.shape[0] // SHELLS
    qbins = radial.shape[1]
    natoms = species.shape[0]
    scale = 1.0 / math.sqrt(npw * nga)
    pair = [(k, k ^ 1) for k in range(nband)]

    sent = pack(coeffs, miller, ndev)
    ra = lax.all_to_all(sent, axes, 0, 0)
    rb = lax.ppermute(ra, "band", pair)

    i = lax.axis_index("ga")
    j = lax.axis_index("band")
    atoms_c = lax.dynamic_slice_in_dim(proj_atom, j * ncols, ncols).reshape(nc, NCH)[:, :1]
    atoms_r = lax.dynamic_slice_in_dim(proj_atom, i * nrows, nrows).reshape(nr, NCH)[:, :1]
    per = -(-SHELLS * kinds // 16) * 16
    table = radial.reshape(kinds, SHELLS, qbins).transpose(1, 0, 2).reshape(SHELLS * kinds, qbins)
    table = jnp.pad(table, ((0, per - SHELLS * kinds), (0, 0)))
    hi = lax.reduce_precision(table, 8, 7)
    mid = lax.reduce_precision(table - hi, 8, 7)
    lo = table - hi - mid
    table = jnp.concatenate([hi, mid, lo], axis=0).astype(jnp.bfloat16)
    width = SPLITS * per
    xc, xr, oc, orr = pl.pallas_call(
        functools.partial(table_kernel, kinds=kinds),
        out_shape=[
            jax.ShapeDtypeStruct((3, nc, LANES), jnp.float32),
            jax.ShapeDtypeStruct((3, nr, LANES), jnp.float32),
            jax.ShapeDtypeStruct((SHELLS, nc, width), jnp.bfloat16),
            jax.ShapeDtypeStruct((SHELLS, nr, width), jnp.bfloat16),
        ],
        name="tables",
    )(atoms_c, atoms_r, species.reshape(1, natoms), positions)

    chunk = row_chunk(nrows)
    vmem = pl.BlockSpec(memory_space=pltpu.VMEM)
    nmax = max(nc, nr)
    own, other = pl.pallas_call(
        functools.partial(
            main_kernel, nband=nband, scale=scale, qscale=(qbins - 1) / (3.0 * MMAX * MMAX), chunk=chunk
        ),
        in_specs=[vmem] * 7 + [pl.BlockSpec(memory_space=pl.ANY)],
        out_specs=[vmem, vmem],
        out_shape=[
            jax.ShapeDtypeStruct((nga, nb // 2, npw), jnp.float32),
            jax.ShapeDtypeStruct((nga, nb // 2, npw), jnp.bfloat16),
        ],
        scratch_shapes=[
            pltpu.VMEM((nrows, ncols), jnp.bfloat16),
            pltpu.SemaphoreType.DMA((nrows // chunk,)),
            pltpu.VMEM((nga, 8, npw), jnp.float32),
            pltpu.VMEM((nga, width, npw), jnp.bfloat16),
            pltpu.VMEM((SHELLS, nmax, npw), jnp.float32),
            pltpu.VMEM((SHELLS * nmax, npw), jnp.bfloat16),
            pltpu.VMEM((SHELLS * nmax, npw), jnp.bfloat16),
            pltpu.VMEM((SHELLS * nc, COMPS * nb), jnp.float32),
            pltpu.VMEM((ncols, nb), jnp.float32),
            pltpu.VMEM((nrows, nb), jnp.float32),
        ],
        compiler_params=pltpu.CompilerParams(vmem_limit_bytes=56 * 1024 * 1024),
        name="apply",
    )(ra, rb, xc, xr, oc, orr, table, coupling)

    theirs = lax.ppermute(other, "band", pair)
    pairs = (own + theirs.astype(jnp.float32)).astype(jnp.bfloat16).reshape(ndev, half, npw)
    back = lax.all_to_all(pairs, axes, 0, 0).reshape(ndev // 2, 2, half, npw)
    return pl.pallas_call(
        finish_kernel,
        out_shape=jax.ShapeDtypeStruct((npw, nbl), jnp.bfloat16),
        name="finish",
    )(back, coeffs)


def solution(mesh):
    placed = (P("ga", "band"), P("ga", "band"), P(None, "ga"), P(), P(), P(), P())
    return jax.shard_map(
        shards, mesh=mesh, in_specs=placed, out_specs=P("ga", "band"), check_vma=False
    )
```

time: 418 us -> 69.9 us (0.17)
  local copies, waits for them, and re-layouts: 181 us -> 7.42 us
  blocking collectives: 114 us -> 32.3 us
  other arithmetic: 37.1 us -> 1.72 us
  loops' own time: 35.3 us -> 0 us
  matrix products: 33.3 us -> 0 us
  Pallas kernels: 0 us -> 25.9 us
  between operations: 13.6 us -> 0.02 us
    psum x1 -> x0, blocking collectives: 82.5 us -> none  [shards(): summed = lax.psum(lax.map(one_block, starts).reshape(NPROJ, nbands), 'ga')]
    gather x64 -> x0, local copies, waits for them, and re-layouts: 59.2 us -> none  [the longest x32 35.9 us: beta_atoms(): place = jnp.take(positions, atoms, axis=1)]
    dynamic_update_slice x32 -> x0, local copies, waits for them, and re-layouts: 53.2 us -> none  [shards(): summed = lax.psum(lax.map(one_block, starts).reshape(NPROJ, nbands), 'ga')]
    another operation x2 -> x0, loops' own time: 35.3 us -> none  [the longest x1 32.7 us: shards(): summed = lax.psum(lax.map(one_block, starts).reshape(NPROJ, nbands), 'ga')]
    dot_general x66 -> x0, matrix products: 33.3 us -> none  [the longest x1 16.8 us: shards(): jnp.dot(full_rows, proj_b, preferred_element_type=jnp.float32)]
    dynamic_slice x48 -> x2, local copies, waits for them, and re-layouts: 34.6 us -> 1.49 us  [the longest x1 0.78 us: shards(): lax.dynamic_slice_in_dim(proj_atom, i * nrows, nrows).reshape(nr, NCH)]
    all_to_all x0 -> x2, blocking collectives: none -> 32.3 us  [the longest x1 19.4 us: shards(): ra = lax.all_to_all(sent, axes, 0, 0)]
    all_gather x1 -> x0, blocking collectives: 32 us -> none  [shards(): lax.all_gather(part, 'ga', axis=0, tiled=True)]
  transfers between devices with their start and end apart: 1 -> 2, of which waited for: 0 -> 1; matrix products, arithmetic and copies ran while one was open for 34% -> 6% of each run, Pallas kernels for 0% -> 5%
where the time goes in v1:
time: 69.9 us; the launch traced here: 69.3 us
  blocking collectives  32.3 us (46%)
  Pallas kernels  25.9 us (37%)
  local copies, waits for them, and re-layouts  7.42 us (11%)
  other arithmetic  1.72 us (2%)
  waiting for transfers between devices  1.38 us (2%)
    all_to_all x1, blocking collectives, shards(): ra = lax.all_to_all(sent, axes, 0, 0)  19.4 us
    pallas_call x1, Pallas kernels, shards(): pl.pallas_call(functools.partial(main_kernel, nband=nband, scale=scale, q...  19.2 us
    all_to_all x1, blocking collectives, shards(): back = lax.all_to_all(pairs, axes, 0, 0).reshape(ndev // 2, 2, half, npw)  13 us
    pallas_call x1, Pallas kernels, shards(): pl.pallas_call(functools.partial(table_kernel, kinds=kinds), out_shape=[j...  3.24 us
    unnamed x5, local copies, waits for them, and re-layouts  2.18 us
    pallas_call x1, Pallas kernels, shards(): pl.pallas_call(finish_kernel, out_shape=jax.ShapeDtypeStruct((npw, nbl),...  1.72 us
    pallas_call x1, Pallas kernels, pack(): pl.pallas_call(pack_kernel, out_shape=jax.ShapeDtypeStruct((ndev // 2, 2,...  1.67 us
    pallas_call x1, local copies, waits for them, and re-layouts, shards(): pl.pallas_call(finish_kernel, out_shape=jax.ShapeDtypeStruct((npw, nbl),...  1.52 us
  transfers between devices with their start and end apart: 2, of which 1 were waited for; matrix products, arithmetic and copies ran while one was open for 6% of the time, Pallas kernels for 5%

profile of v1, /device:TPU:0, one launch (start us, length us, event | category | flops | bytes accessed | tf_op | source)
XLA Modules:
  0.0 69.3 jit_solution(5211498345250336394)
XLA Ops:
  0.0 1.5 %copy.12.coef_ref = bf16[256,32]{1,0:T(8,128)(2,1)} copy(bf16[256,32]{0,1:T(8,128)(2,1)} %param.7) | data formatting | bytes 32768 | tf_op args[0]
  1.5 1.7 %pack.1 = bf16[16,2,40,128]{3,2,1,0:T(8,128)(2,1)} custom-call(bf16[256,32]{1,0:T(8,128)(2,1)} %copy.12.coef_ref, s32[3,256]{1,0:T(4,128)} %mil_ref.1), custom_call_target="tpu_custom_call" | custom-call | tf_op jit(solution)/shard_map/pack/pallas_call | solution.py:74
  3.1 19.4 %all_to_all.10.ra_ref = bf16[32,40,128]{2,1,0:T(8,128)(2,1)S(1)} all-to-all(bf16[32,40,128]{2,1,0:T(8,128)(2,1)} %bitcast.7), channel_id=1, replica_groups=mesh['ga'=8,'band'=4] {'ga','band'}, dimensions={0} | all-to-all | bytes 655360 | tf_op jit(solution)/shard_map/all_to_all | solution.py:260
  22.5 0.0 copy-start
  22.5 0.0 collective-permute-start
  22.5 0.7 %reshape.28 = f32[4,3,128]{2,1,0:T(4,128)S(1)} reshape(f32[12,128]{1,0:T(8,128)} %param.13) | data formatting | bytes 12288 | tf_op jit(solution)/shard_map/reshape | solution.py:268
  23.2 0.8 %dynamic_slice.7 = s32[1536]{0:T(1024)S(1)} dynamic-slice(s32[12288]{0:T(1024)} %param.11, s32[]{:T(128)S(6)} %select_n.7), dynamic_slice_sizes={1536} | dynamic-slice | bytes 12292 | tf_op jit(solution)/shard_map/dynamic_slice | solution.py:266
  24.0 0.7 %dynamic_slice.6 = s32[3072]{0:T(1024)S(1)} dynamic-slice(s32[12288]{0:T(1024)} %param.11, s32[]{:T(128)S(6)} %select_n.6), dynamic_slice_sizes={3072} | dynamic-slice | bytes 24580 | tf_op jit(solution)/shard_map/dynamic_slice | solution.py:265
  24.7 0.7 %reshape.26 = s32[128,12]{1,0:T(8,128)} reshape(s32[1536]{0:T(1024)S(1)} %dynamic_slice.7) | data formatting | bytes 12288 | tf_op jit(solution)/shard_map/reshape | solution.py:266
  25.4 0.8 %reshape.25 = s32[256,12]{1,0:T(8,128)} reshape(s32[3072]{0:T(1024)S(1)} %dynamic_slice.6) | data formatting | bytes 24576 | tf_op jit(solution)/shard_map/reshape | solution.py:265
  26.2 3.2 %tables.1 = (f32[3,256,128]{2,1,0:T(8,128)}, f32[3,128,128]{2,1,0:T(8,128)}, bf16[3,256,48]{2,1,0:T(8,128)(2,1)}, bf16[3,128,48]{2,1,0:T(8,128)(2,1)}) custom-call(s32[256,1]{1,0:T(8,128)} %bitcast.10, s32[128,1]{1,0:T(8,128)} %bitcast.11, s32[1,1024]{1,0:T(1,128)} %bitcast.13, f32[3,1024]{1,0:T(4,128)} %pos_ref.1), custom_call_target="tpu_custom_call" | custom-call | tf_op jit(solution)/shard_map/tables/pallas_call | solution.py:275
  29.5 0.6 pad_maximum_fusion.rad_ref
  30.1 0.0 collective-permute-done.rb_ref
  30.1 0.0 copy-start.1
  30.1 0.0 copy-done
  30.1 0.7 %copy-done.1 = bf16[32,40,128]{2,1,0:T(8,128)(2,1)} copy-done((bf16[32,40,128]{2,1,0:T(8,128)(2,1)}, bf16[32,40,128]{2,1,0:T(8,128)(2,1)S(1)}, u32[]{:S(2)}) %copy-start.1) | copy-done | bytes 327704
  30.8 19.2 %apply.1 = (f32[8,64,256]{2,1,0:T(8,128)}, bf16[8,64,256]{2,1,0:T(8,128)(2,1)}) custom-call(bf16[32,40,128]{2,1,0:T(8,128)(2,1)} %copy-done, bf16[32,40,128]{2,1,0:T(8,128)(2,1)} %copy-done.1, f32[3,256,128]{2,1,0:T(8,128)} %get-tuple-element.11.xc_ref, f32[3,128,128]{2,1,0:T(8,128)} %get-tuple-element.12.xr_ref, ...), custom_call_target="tpu_custom_call" | custom-call | tf_op jit(solution)/shard_map/apply/pallas_call | solution.py:289
  50.1 0.6 collective-permute-start.1
  50.6 1.4 %collective-permute-done.1 = bf16[8,64,256]{2,1,0:T(8,128)(2,1)S(1)} collective-permute-done((bf16[8,64,256]{2,1,0:T(8,128)(2,1)}, bf16[8,64,256]{2,1,0:T(8,128)(2,1)S(1)}, u32[]{:S(2)}, u32[]{:S(2)}) %collective-permute-start.1) | collective-permute-done | bytes 262176 | tf_op jit(solution)/shard_map/ppermute | solution.py:315
  52.0 1.1 %add_convert_fusion = bf16[8,64,256]{2,1,0:T(8,128)(2,1)S(1)} fusion(f32[8,64,256]{2,1,0:T(8,128)} %get-tuple-element.15, bf16[8,64,256]{2,1,0:T(8,128)(2,1)S(1)} %collective-permute-done.1), kind=kLoop, calls=%fused_computation | loop fusion | flops 393216 | bytes 1048576 | tf_op jit(solution)/shard_map/convert_element_type | solution.py:316
  53.1 13.0 %all_to_all.11 = bf16[32,16,256]{2,1,0:T(8,128)(2,1)} all-to-all(bf16[32,16,256]{2,1,0:T(8,128)(2,1)S(1)} %bitcast.9), channel_id=1, replica_groups=mesh['ga'=8,'band'=4] {'ga','band'}, dimensions={0} | all-to-all | bytes 524288 | tf_op jit(solution)/shard_map/all_to_all | solution.py:317
  66.1 1.7 %finish.1 = bf16[256,32]{1,0:T(8,128)(2,1)} custom-call(bf16[16,2,16,256]{3,2,1,0:T(8,128)(2,1)} %bitcast.8, bf16[256,32]{1,0:T(8,128)(2,1)} %copy.12.coef_ref), custom_call_target="tpu_custom_call" | custom-call | tf_op jit(solution)/shard_map/finish/pallas_call | solution.py:318
  67.8 1.5 %copy.15 = bf16[256,32]{0,1:T(8,128)(2,1)} copy(bf16[256,32]{1,0:T(8,128)(2,1)} %finish.1) | data formatting | bytes 32768 | tf_op jit(solution)/shard_map/finish/pallas_call | solution.py:318
  (3 shorter events, 0.0 us)
Async XLA Ops:
  22.5 7.6 %copy-start = (bf16[32,40,128]{2,1,0:T(8,128)(2,1)}, bf16[32,40,128]{2,1,0:T(8,128)(2,1)S(1)}, u32[]{:S(2)}) copy-start(bf16[32,40,128]{2,1,0:T(8,128)(2,1)S(1)} %all_to_all.10.ra_ref) | copy-start | bytes 983044
  22.5 7.6 %collective-permute-start = (bf16[32,40,128]{2,1,0:T(8,128)(2,1)S(1)}, bf16[32,40,128]{2,1,0:T(8,128)(2,1)S(1)}, u32[]{:S(2)}, u32[]{:S(2)}) collective-permute-start(bf16[32,40,128]{2,1,0:T(8,128)(2,1)S(1)} %all_to_all.10.ra_ref), channel_id=1, source_target_pairs={{0,1},{1,0},{2,3},{3,2},{4,5},{5,4},{6,7},{7,6},{8,9},{9,8},{10,11... | collective-permute-start | bytes 983048 | tf_op jit(solution)/shard_map/ppermute | solution.py:261
  30.1 0.7 %copy-start.1 = (bf16[32,40,128]{2,1,0:T(8,128)(2,1)}, bf16[32,40,128]{2,1,0:T(8,128)(2,1)S(1)}, u32[]{:S(2)}) copy-start(bf16[32,40,128]{2,1,0:T(8,128)(2,1)S(1)} %collective-permute-done.rb_ref) | copy-start | bytes 983044
  50.1 1.9 %collective-permute-start.1 = (bf16[8,64,256]{2,1,0:T(8,128)(2,1)}, bf16[8,64,256]{2,1,0:T(8,128)(2,1)S(1)}, u32[]{:S(2)}, u32[]{:S(2)}) collective-permute-start(bf16[8,64,256]{2,1,0:T(8,128)(2,1)} %get-tuple-element.16), channel_id=1, source_target_pairs={{0,1},{1,0},{2,3},{3,2},{4,5},{5,4},{6,7},{7,6},{8,9},{9,8},{10,11... | collective-permute-start | bytes 786440 | tf_op jit(solution)/shard_map/ppermute | solution.py:315

commit v2 on v1

--- a/solution.py
+++ b/solution.py
@@ -51,31 +51,32 @@
 
 
 def pack_kernel(coef_ref, mil_ref, out_ref):
-    half = coef_ref.shape[1] // 2
-    npw = coef_ref.shape[0]
-    ct = coef_ref[...].astype(jnp.float32).T
+    half = coef_ref.shape[0] // 2
+    ngroups = coef_ref.shape[1] // LANES
     m = mil_ref[...].astype(jnp.float32)
-    ngroups = npw // LANES
     mrows = [m[c : c + 1, g * LANES : (g + 1) * LANES] for c in range(3) for g in range(ngroups)]
-    used = len(mrows)
-    pad = out_ref.shape[2] - half * ngroups - used
+    pad = out_ref.shape[2] - half * ngroups - len(mrows)
     if pad:
         mrows.append(jnp.zeros((pad, LANES), jnp.float32))
+    mblock = jnp.concatenate(mrows, axis=0).astype(jnp.bfloat16)
     for h in range(2):
-        rows = [ct[h * half : (h + 1) * half, g * LANES : (g + 1) * LANES] for g in range(ngroups)]
-        block = jnp.concatenate(rows + mrows, axis=0).astype(jnp.bfloat16)
-        out_ref[:, h] = jnp.broadcast_to(block[None], (out_ref.shape[0],) + block.shape)
-
-
-def pack(coeffs, miller, ndev):
-    npw, nbl = coeffs.shape
+        rows = [
+            coef_ref[h * half : (h + 1) * half, g * LANES : (g + 1) * LANES] for g in range(ngroups)
+        ]
+        block = jnp.concatenate(rows + [mblock], axis=0)
+        for d in range(out_ref.shape[0]):
+            out_ref[d, h] = block
+
+
+def pack(coeffs_t, miller, ndev):
+    nbl, npw = coeffs_t.shape
     ngroups = npw // LANES
     rows = -(-(nbl // 2 * ngroups + 3 * ngroups) // 8) * 8
     out = pl.pallas_call(
         pack_kernel,
         out_shape=jax.ShapeDtypeStruct((ndev // 2, 2, rows, LANES), jnp.bfloat16),
         name="pack",
-    )(coeffs, miller)
+    )(coeffs_t, miller)
     return out.reshape(ndev, rows, LANES)
 
 
@@ -99,8 +100,9 @@
 
 def main_kernel(
     ra_ref, rb_ref, xc_ref, xr_ref, oc_ref, or_ref, rad_ref, b_hbm, own_ref, oth_ref,
-    b_ref, sem, ms_ref, rads_ref, sel_ref, gc_ref, gs_ref, acc_ref, proj_ref, mix_ref,
-    *, nband, scale, qscale, chunk,
+    b_ref, sem, ms_ref, rads_ref, sel_ref, gca_ref, gsa_ref, cf_ref, acc_ref, proj_ref, mix_ref,
+    gcc_ref, gsc_ref,
+    *, nband, scale, qscale, chunk, group,
 ):
     nga = ms_ref.shape[0]
     npw = ms_ref.shape[2]
@@ -112,6 +114,7 @@
     nrows = b_ref.shape[0]
     qbins = rad_ref.shape[1]
     per = rads_ref.shape[1] // SPLITS
+    nsteps = nga // group
 
     copies = [
         pltpu.make_async_copy(b_hbm.at[pl.ds(k * chunk, chunk)], b_ref.at[pl.ds(k * chunk, chunk)], sem.at[k])
@@ -120,14 +123,14 @@
     for copy in copies:
         copy.start()
 
-    def prepare(i, carry):
+    def prepare(i):
         raw = ra_ref[i * nband, half * ngroups :, :].astype(jnp.float32)
         comps = [
             jnp.concatenate([raw[c * ngroups + g : c * ngroups + g + 1] for g in range(ngroups)], axis=1)
             for c in range(3)
         ]
-        m = jnp.concatenate(comps + [jnp.zeros((5, npw), jnp.float32)], axis=0)
-        ms_ref[i] = m
+        for c in range(3):
+            ms_ref[i, c : c + 1, :] = comps[c]
         q = (comps[0] * comps[0] + comps[1] * comps[1] + comps[2] * comps[2]) * jnp.float32(qscale)
         knot = lax.broadcasted_iota(jnp.int32, (qbins, npw), 0).astype(jnp.float32)
         hats = jnp.maximum(0.0, 1.0 - jnp.abs(q - knot))
@@ -137,14 +140,11 @@
         r = nn_dot(table, hi) + nn_dot(table, lo)
         r = (r[0:per] + r[per : 2 * per] + r[2 * per : 3 * per]) * jnp.float32(scale)
         rads_ref[i] = jnp.concatenate(split3(r), axis=0)
-        return carry
-
-    lax.fori_loop(0, nga, prepare, 0)
-
-    def build(i, x_ref, o_ref, n):
+
+    def build(i, x_ref, o_ref, n, sel, put):
         rads = rads_ref[i]
         for s in range(SHELLS):
-            sel_ref[s, :n] = nn_dot(o_ref[s], rads)
+            sel[s, :n] = nn_dot(o_ref[s], rads)
         m = [ms_ref[i, c : c + 1, :] for c in range(3)]
         step = 16 if n % 16 == 0 else n
         for a in range(0, n, step):
@@ -154,9 +154,8 @@
                 turns = turns + jnp.concatenate([x] * ngroups, axis=1) * m[c]
             cos, sin = cos_sin_turns(turns)
             for s in range(SHELLS):
-                sel = sel_ref[s, a : a + step, :]
-                gc_ref[s * n + a : s * n + a + step, :] = (sel * cos).astype(jnp.bfloat16)
-                gs_ref[s * n + a : s * n + a + step, :] = (sel * sin).astype(jnp.bfloat16)
+                v = sel[s, a : a + step, :]
+                put(s * n + a, step, (v * cos).astype(jnp.bfloat16), (v * sin).astype(jnp.bfloat16))
 
     def weights(i):
         return [ms_ref[i, c : c + 1, :] * jnp.float32(1.0 / MMAX) for c in range(3)]
@@ -172,20 +171,57 @@
                 )
         return jnp.concatenate(rows, axis=0)
 
-    acc_ref[...] = jnp.zeros(acc_ref.shape, jnp.float32)
-
-    def project(i, carry):
-        build(i, xc_ref, oc_ref, nc)
-        c = coefs(i)
-        cf = c.astype(jnp.float32)
-        w = weights(i)
-        wc = jnp.concatenate([(cf * w[k]).astype(jnp.bfloat16) for k in range(3)], axis=0)
-        rows = SHELLS * nc
-        acc_ref[:, :nb] += nt_dot(gc_ref[:rows, :], c)
-        acc_ref[:, nb:] += nt_dot(gs_ref[:rows, :], wc)
+    def stage(step, slot):
+        for e in range(group):
+            i = step * group + e
+            lanes = slice(e * npw, (e + 1) * npw)
+
+            def put(row, count, c, s, lanes=lanes):
+                gca_ref[slot, row : row + count, lanes] = c
+                gsa_ref[slot, row : row + count, lanes] = s
+
+            prepare(i)
+            build(i, xc_ref, oc_ref, nc, sel_ref.at[slot], put)
+            c = coefs(i)
+            cf = c.astype(jnp.float32)
+            w = weights(i)
+            cf_ref[slot, :nb, lanes] = c
+            for k in range(3):
+                cf_ref[slot, (k + 1) * nb : (k + 2) * nb, lanes] = (cf * w[k]).astype(jnp.bfloat16)
+
+    def consume(slot):
+        acc_ref[:, :nb] += nt_dot(gca_ref[slot], cf_ref[slot, :nb])
+        acc_ref[:, nb:] += nt_dot(gsa_ref[slot], cf_ref[slot, nb:])
+
+    def clear(k, carry):
+        acc_ref[pl.ds(pl.multiple_of(k * nc, 8), nc), :] = jnp.zeros((nc, acc_ref.shape[1]), jnp.float32)
         return carry
 
-    lax.fori_loop(0, nga, project, 0)
+    lax.fori_loop(0, SHELLS, clear, 0)
+    stage(0, 0)
+    if nsteps <= 8:
+        for step in range(1, nsteps):
+            stage(step, step % 2)
+            consume((step - 1) % 2)
+    else:
+        def body(step, carry):
+            slot = step % 2
+            stage(step, slot)
+            consume(1 - slot)
+            return carry
+
+        lax.fori_loop(1, nsteps, body, 0)
+    def rebuild(i, slot):
+        def put(row, count, c, s):
+            gcc_ref[i, row : row + count, :] = c
+            gsc_ref[i, row : row + count, :] = s
+
+        build(i, xr_ref, or_ref, nr, sel_ref.at[slot], put)
+
+    early = 4 if nga <= 16 else 0
+    for i in range(early):
+        rebuild(i, i % 2)
+    consume((nsteps - 1) % 2)
 
     for s in range(SHELLS):
         for t in range(COMPS):
@@ -194,9 +230,26 @@
             ]
     proj = proj_ref[...].astype(jnp.bfloat16)
 
-    for k, copy in enumerate(copies):
+    def multiply(first, count):
+        mix_ref[first : first + count, :] = nn_dot(b_ref[first : first + count, :], proj)
+
+    for copy in copies:
         copy.wait()
-        mix_ref[k * chunk : (k + 1) * chunk, :] = nn_dot(b_ref[k * chunk : (k + 1) * chunk, :], proj)
+    nmul = nrows // chunk
+    if nga <= 16:
+        for k in range(nmul):
+            multiply(k * chunk, chunk)
+            for i in range(early + k * (nga - early) // nmul, early + (k + 1) * (nga - early) // nmul):
+                rebuild(i, i % 2)
+    else:
+        for k in range(nmul):
+            multiply(k * chunk, chunk)
+
+        def again(i, carry):
+            rebuild(i, i % 2)
+            return carry
+
+        lax.fori_loop(0, nga, again, 0)
 
     mixed = []
     for t in range(COMPS):
@@ -207,23 +260,28 @@
     m0 = mixed[0].astype(jnp.bfloat16)
     mt = jnp.concatenate(mixed[1:], axis=0).astype(jnp.bfloat16)
 
-    def expand(i, carry):
-        build(i, xr_ref, or_ref, nr)
-        rows = SHELLS * nr
-        y = nn_dot(m0, gc_ref[:rows, :])
-        ys = nn_dot(mt, gs_ref[:rows, :])
+    def expand(i):
+        y = nn_dot(m0, gcc_ref[i])
+        ys = nn_dot(mt, gsc_ref[i])
         w = weights(i)
         for k in range(3):
             y = y + w[k] * ys[k * nb : (k + 1) * nb]
         own_ref[i] = y[: nb // 2]
         oth_ref[i] = y[nb // 2 :].astype(jnp.bfloat16)
-        return carry
-
-    lax.fori_loop(0, nga, expand, 0)
+
+    if nga <= 16:
+        for i in range(nga):
+            expand(i)
+    else:
+        def body(i, carry):
+            expand(i)
+            return carry
+
+        lax.fori_loop(0, nga, body, 0)
 
 
 def row_chunk(count):
-    for cand in range(min(count, 512), 0, -1):
+    for cand in range(min(count, 256), 0, -1):
         if count % cand == 0 and cand % 8 == 0:
             return cand
     return count
@@ -236,7 +294,7 @@
         def add(k, acc, h=h):
             return acc + recv_ref[k, h].astype(jnp.float32)
         parts.append(lax.fori_loop(0, n, add, jnp.zeros(recv_ref.shape[2:], jnp.float32), unroll=8))
-    total = jnp.concatenate(parts, axis=0).T
+    total = jnp.concatenate(parts, axis=0)
     out_ref[...] = (coef_ref[...].astype(jnp.float32) + total).astype(out_ref.dtype)
 
 
@@ -256,10 +314,9 @@
     scale = 1.0 / math.sqrt(npw * nga)
     pair = [(k, k ^ 1) for k in range(nband)]
 
-    sent = pack(coeffs, miller, ndev)
+    coeffs_t = coeffs.T
+    sent = pack(coeffs_t, miller, ndev)
     ra = lax.all_to_all(sent, axes, 0, 0)
-    rb = lax.ppermute(ra, "band", pair)
-
     i = lax.axis_index("ga")
     j = lax.axis_index("band")
     atoms_c = lax.dynamic_slice_in_dim(proj_atom, j * ncols, ncols).reshape(nc, NCH)[:, :1]
@@ -280,15 +337,22 @@
             jax.ShapeDtypeStruct((SHELLS, nc, width), jnp.bfloat16),
             jax.ShapeDtypeStruct((SHELLS, nr, width), jnp.bfloat16),
         ],
+        cost_estimate=pl.CostEstimate(flops=10**9, transcendentals=0, bytes_accessed=10**6),
+        compiler_params=pltpu.CompilerParams(vmem_limit_bytes=16 * 1024 * 1024),
         name="tables",
     )(atoms_c, atoms_r, species.reshape(1, natoms), positions)
+
+    ra, table, xc, xr, oc, orr = lax.optimization_barrier((ra, table, xc, xr, oc, orr))
+    rb = lax.ppermute(ra, "band", pair)
 
     chunk = row_chunk(nrows)
     vmem = pl.BlockSpec(memory_space=pltpu.VMEM)
     nmax = max(nc, nr)
+    group = 2 if nga % 2 == 0 else 1
     own, other = pl.pallas_call(
         functools.partial(
-            main_kernel, nband=nband, scale=scale, qscale=(qbins - 1) / (3.0 * MMAX * MMAX), chunk=chunk
+            main_kernel, nband=nband, scale=scale, qscale=(qbins - 1) / (3.0 * MMAX * MMAX), chunk=chunk,
+            group=group,
         ),
         in_specs=[vmem] * 7 + [pl.BlockSpec(memory_space=pl.ANY)],
         out_specs=[vmem, vmem],
@@ -301,14 +365,17 @@
             pltpu.SemaphoreType.DMA((nrows // chunk,)),
             pltpu.VMEM((nga, 8, npw), jnp.float32),
             pltpu.VMEM((nga, width, npw), jnp.bfloat16),
-            pltpu.VMEM((SHELLS, nmax, npw), jnp.float32),
-            pltpu.VMEM((SHELLS * nmax, npw), jnp.bfloat16),
-            pltpu.VMEM((SHELLS * nmax, npw), jnp.bfloat16),
+            pltpu.VMEM((2, SHELLS, nmax, npw), jnp.float32),
+            pltpu.VMEM((2, SHELLS * nc, group * npw), jnp.bfloat16),
+            pltpu.VMEM((2, SHELLS * nc, group * npw), jnp.bfloat16),
+            pltpu.VMEM((2, COMPS * nb, group * npw), jnp.bfloat16),
             pltpu.VMEM((SHELLS * nc, COMPS * nb), jnp.float32),
             pltpu.VMEM((ncols, nb), jnp.float32),
             pltpu.VMEM((nrows, nb), jnp.float32),
+            pltpu.VMEM((nga, SHELLS * nr, npw), jnp.bfloat16),
+            pltpu.VMEM((nga, SHELLS * nr, npw), jnp.bfloat16),
         ],
-        compiler_params=pltpu.CompilerParams(vmem_limit_bytes=56 * 1024 * 1024),
+        compiler_params=pltpu.CompilerParams(vmem_limit_bytes=50 * 1024 * 1024),
         name="apply",
     )(ra, rb, xc, xr, oc, orr, table, coupling)
 
@@ -317,9 +384,10 @@
     back = lax.all_to_all(pairs, axes, 0, 0).reshape(ndev // 2, 2, half, npw)
     return pl.pallas_call(
         finish_kernel,
-        out_shape=jax.ShapeDtypeStruct((npw, nbl), jnp.bfloat16),
+        out_shape=jax.ShapeDtypeStruct((nbl, npw), jnp.bfloat16),
+        compiler_params=pltpu.CompilerParams(vmem_limit_bytes=16 * 1024 * 1024),
         name="finish",
-    )(back, coeffs)
+    )(back, coeffs_t).T
 
 
 def solution(mesh):

time: 69.9 us -> 49 us (0.70)
  blocking collectives: 32.3 us -> 12.7 us
  Pallas kernels: 25.9 us -> 14.5 us
  waiting for transfers between devices: 1.38 us -> 9.63 us
  starting transfers between devices: 0.57 us -> 7.53 us
  local copies, waits for them, and re-layouts: 7.42 us -> 3.85 us
  other arithmetic: 1.72 us -> 0.08 us
    all_to_all x1 -> x0, blocking collectives: 19.4 us -> none  [shards(): ra = lax.all_to_all(sent, axes, 0, 0)]
    pallas_call x1, Pallas kernels: 19.2 us -> 10.8 us  [shards(): pl.pallas_call(functools.partial(main_kernel, nband=nband, scale=scale, q...]
    all_to_all x0 -> x1, starting transfers between devices: none -> 7.33 us  [shards(): ra = lax.all_to_all(sent, axes, 0, 0)]
    all_to_all x0 -> x1, waiting for transfers between devices: none -> 6.61 us  [shards(): ra = lax.all_to_all(sent, axes, 0, 0)]
    pallas_call x1, Pallas kernels: 3.24 us -> 1.51 us  [shards(): pl.pallas_call(functools.partial(table_kernel, kinds=kinds), out_shape=[j...]
    ppermute x1, waiting for transfers between devices: 0.01 us -> 1.63 us  [shards(): rb = lax.ppermute(ra, 'band', pair)]
    pallas_call x1 -> x0, local copies, waits for them, and re-layouts: 1.52 us -> none  [shards(): pl.pallas_call(finish_kernel, out_shape=jax.ShapeDtypeStruct((npw, nbl),...]
    pallas_call x1, Pallas kernels: 1.72 us -> 0.65 us  [shards(): pl.pallas_call(finish_kernel, out_shape=jax.ShapeDtypeStruct((nbl, npw),...]
  transfers between devices with their start and end apart: 2 -> 3, of which waited for: 1 -> 3; matrix products, arithmetic and copies ran while one was open for 6% -> 5% of each run, Pallas kernels for 5% -> 3%
where the time goes in v2:
time: 49 us; the launch traced here: 48.4 us
  Pallas kernels  14.5 us (30%)
  blocking collectives  12.7 us (26%)
  waiting for transfers between devices  9.63 us (20%)
  starting transfers between devices  7.53 us (15%)
  local copies, waits for them, and re-layouts  3.85 us (8%)
    all_to_all x1, blocking collectives, shards(): back = lax.all_to_all(pairs, axes, 0, 0).reshape(ndev // 2, 2, half, npw)  12.7 us
    pallas_call x1, Pallas kernels, shards(): pl.pallas_call(functools.partial(main_kernel, nband=nband, scale=scale, q...  10.8 us
    all_to_all x1, starting transfers between devices, shards(): ra = lax.all_to_all(sent, axes, 0, 0)  7.33 us
    all_to_all x1, waiting for transfers between devices, shards(): ra = lax.all_to_all(sent, axes, 0, 0)  6.61 us
    ppermute x1, waiting for transfers between devices, shards(): rb = lax.ppermute(ra, 'band', pair)  1.63 us
    pallas_call x1, Pallas kernels, pack(): pl.pallas_call(pack_kernel, out_shape=jax.ShapeDtypeStruct((ndev // 2, 2,...  1.55 us
    pallas_call x1, Pallas kernels, shards(): pl.pallas_call(functools.partial(table_kernel, kinds=kinds), out_shape=[j...  1.51 us
    unnamed x6, local copies, waits for them, and re-layouts  1.4 us
  transfers between devices with their start and end apart: 3, of which 3 were waited for; matrix products, arithmetic and copies ran while one was open for 5% of the time, Pallas kernels for 3%

profile of v2, /device:TPU:0, one launch (start us, length us, event | category | flops | bytes accessed | tf_op | source)
XLA Modules:
  0.0 48.4 jit_solution(13991033872725090511)
XLA Ops:
  0.0 0.0 copy-start
  0.0 1.5 %pack.1 = bf16[16,2,40,128]{3,2,1,0:T(8,128)(2,1)} custom-call(bf16[32,256]{1,0:T(8,128)(2,1)} %bitcast.11, s32[3,256]{1,0:T(4,128)} %mil_ref.1), custom_call_target="tpu_custom_call" | custom-call | tf_op jit(solution)/shard_map/pack/pallas_call | solution.py:75
  1.6 7.3 %all-to-all-start = ((bf16[32,40,128]{2,1,0:T(8,128)(2,1)}), bf16[32,40,128]{2,1,0:T(8,128)(2,1)S(1)}, u32[]{:S(2)}, u32[]{:S(2)}) async-start(bf16[32,40,128]{2,1,0:T(8,128)(2,1)} %bitcast.15), calls=%async_computation | async-start | bytes 655360 | tf_op jit(solution)/shard_map/all_to_all | solution.py:319
  8.9 0.7 %reshape.25 = f32[4,3,128]{2,1,0:T(4,128)S(1)} reshape(f32[12,128]{1,0:T(8,128)} %param.13) | data formatting | bytes 12288 | tf_op jit(solution)/shard_map/reshape | solution.py:325
  9.6 0.8 %dynamic_slice.7 = s32[1536]{0:T(1024)S(1)} dynamic-slice(s32[12288]{0:T(1024)} %param.11, s32[]{:T(128)S(6)} %select_n.7), dynamic_slice_sizes={1536} | dynamic-slice | bytes 12292 | tf_op jit(solution)/shard_map/dynamic_slice | solution.py:323
  10.4 0.7 %dynamic_slice.6 = s32[3072]{0:T(1024)S(1)} dynamic-slice(s32[12288]{0:T(1024)} %param.11, s32[]{:T(128)S(6)} %select_n.6), dynamic_slice_sizes={3072} | dynamic-slice | bytes 24580 | tf_op jit(solution)/shard_map/dynamic_slice | solution.py:322
  11.1 0.1 reshape.28
  11.2 0.1 reshape.27
  11.4 0.0 copy-start.1
  11.4 0.7 %copy-done.1 = f32[3,1024]{1,0:T(4,128)S(1)} copy-done((f32[3,1024]{1,0:T(4,128)S(1)}, f32[3,1024]{1,0:T(4,128)}, u32[]{:S(2)}) %copy-start.1) | copy-done | bytes 12312
  12.1 0.0 copy-start.2
  12.1 0.7 %copy-done.2 = s32[1024]{0:T(1024)S(1)} copy-done((s32[1024]{0:T(1024)S(1)}, s32[1024]{0:T(1024)}, u32[]{:S(2)}) %copy-start.2) | copy-done | bytes 4120
  12.8 1.5 %tables.1 = (f32[3,256,128]{2,1,0:T(8,128)S(1)}, f32[3,128,128]{2,1,0:T(8,128)S(1)}, bf16[3,256,48]{2,1,0:T(8,128)(2,1)S(1)}, bf16[3,128,48]{2,1,0:T(8,128)(2,1)S(1)}) custom-call(s32[256,1]{1,0:T(8,128)S(1)} %bitcast.10, s32[128,1]{1,0:T(8,128)S(1)} %bitcast.13, s32[1,1024]{1,0:T(1,128)S(1)} %bitcast.14, f32[3,1024]{1,0:T(4,128)S(1)} %copy-done.1), custom_call_target="tpu_custom_call" | custom-call | flops 1000000000 | bytes 1000000 | tf_op jit(solution)/shard_map/tables/pallas_call | solution.py:332
  14.3 6.6 %all-to-all-done.ra_ref = bf16[32,40,128]{2,1,0:T(8,128)(2,1)S(1)} async-done(((bf16[32,40,128]{2,1,0:T(8,128)(2,1)}), bf16[32,40,128]{2,1,0:T(8,128)(2,1)S(1)}, u32[]{:S(2)}, u32[]{:S(2)}) %all-to-all-start) | async-done | bytes 327712 | tf_op jit(solution)/shard_map/all_to_all | solution.py:319
  20.9 0.0 collective-permute-start
  20.9 1.6 %collective-permute-done.rb_ref = bf16[32,40,128]{2,1,0:T(8,128)(2,1)S(1)} collective-permute-done((bf16[32,40,128]{2,1,0:T(8,128)(2,1)S(1)}, bf16[32,40,128]{2,1,0:T(8,128)(2,1)S(1)}, u32[]{:S(2)}, u32[]{:S(2)}) %collective-permute-start) | collective-permute-done | bytes 327712 | tf_op jit(solution)/shard_map/ppermute | solution.py:346
  22.6 10.8 %apply.1 = (f32[8,64,256]{2,1,0:T(8,128)S(1)}, bf16[8,64,256]{2,1,0:T(8,128)(2,1)S(1)}) custom-call(bf16[32,40,128]{2,1,0:T(8,128)(2,1)S(1)} %all-to-all-done.ra_ref, bf16[32,40,128]{2,1,0:T(8,128)(2,1)S(1)} %collective-permute-done.rb_ref, f32[3,256,128]{2,1,0:T(8,128)S(1)} %get-tuple-element.22.xc_ref, f32[3,128,128]{2,1,0:T(8,128)S(1)} %get-tuple-element.23.xr_ref, ...), custom_call_target="tpu_custom_call" | custom-call | tf_op jit(solution)/shard_map/apply/pallas_call | solution.py:352
  33.4 0.2 collective-permute-start.1
  33.6 1.4 %collective-permute-done.1 = bf16[8,64,256]{2,1,0:T(8,128)(2,1)S(1)} collective-permute-done((bf16[8,64,256]{2,1,0:T(8,128)(2,1)S(1)}, bf16[8,64,256]{2,1,0:T(8,128)(2,1)S(1)}, u32[]{:S(2)}, u32[]{:S(2)}) %collective-permute-start.1) | collective-permute-done | bytes 262176 | tf_op jit(solution)/shard_map/ppermute | solution.py:382
  35.0 0.1 add_convert_fusion
  35.0 12.7 %all_to_all.10 = bf16[32,16,256]{2,1,0:T(8,128)(2,1)S(1)} all-to-all(bf16[32,16,256]{2,1,0:T(8,128)(2,1)S(1)} %bitcast.16), channel_id=1, replica_groups=mesh['ga'=8,'band'=4] {'ga','band'}, dimensions={0} | all-to-all | bytes 524288 | tf_op jit(solution)/shard_map/all_to_all | solution.py:384
  47.7 0.0 copy-done
  47.7 0.7 %finish.1 = bf16[32,256]{1,0:T(8,128)(2,1)} custom-call(bf16[16,2,16,256]{3,2,1,0:T(8,128)(2,1)S(1)} %bitcast.9, bf16[32,256]{1,0:T(8,128)(2,1)S(1)} %bitcast.12), custom_call_target="tpu_custom_call" | custom-call | tf_op jit(solution)/shard_map/finish/pallas_call | solution.py:385
  (4 shorter events, 0.0 us)
Async XLA Ops:
  0.0 47.7 %copy-start = (bf16[256,32]{0,1:T(8,128)(2,1)S(1)}, bf16[256,32]{0,1:T(8,128)(2,1)}, u32[]{:S(2)}) copy-start(bf16[256,32]{0,1:T(8,128)(2,1)} %param.7) | copy-start | bytes 49156
  1.6 19.4 %all-to-all-start = ((bf16[32,40,128]{2,1,0:T(8,128)(2,1)}), bf16[32,40,128]{2,1,0:T(8,128)(2,1)S(1)}, u32[]{:S(2)}, u32[]{:S(2)}) async-start(bf16[32,40,128]{2,1,0:T(8,128)(2,1)} %bitcast.15), calls=%async_computation | async-start | bytes 655360 | tf_op jit(solution)/shard_map/all_to_all | solution.py:319
  11.4 0.7 %copy-start.1 = (f32[3,1024]{1,0:T(4,128)S(1)}, f32[3,1024]{1,0:T(4,128)}, u32[]{:S(2)}) copy-start(f32[3,1024]{1,0:T(4,128)} %pos_ref.1) | copy-start | bytes 36868
  12.1 0.7 %copy-start.2 = (s32[1024]{0:T(1024)S(1)}, s32[1024]{0:T(1024)}, u32[]{:S(2)}) copy-start(s32[1024]{0:T(1024)} %param.10) | copy-start | bytes 12292
  20.9 1.6 %collective-permute-start = (bf16[32,40,128]{2,1,0:T(8,128)(2,1)S(1)}, bf16[32,40,128]{2,1,0:T(8,128)(2,1)S(1)}, u32[]{:S(2)}, u32[]{:S(2)}) collective-permute-start(bf16[32,40,128]{2,1,0:T(8,128)(2,1)S(1)} %all-to-all-done.ra_ref), channel_id=1, source_target_pairs={{0,1},{1,0},{2,3},{3,2},{4,5},{5,4},{6,7},{7,6},{8,9},{9,8},{10,11... | collective-permute-start | bytes 983048 | tf_op jit(solution)/shard_map/ppermute | solution.py:346
  33.4 1.6 %collective-permute-start.1 = (bf16[8,64,256]{2,1,0:T(8,128)(2,1)S(1)}, bf16[8,64,256]{2,1,0:T(8,128)(2,1)S(1)}, u32[]{:S(2)}, u32[]{:S(2)}) collective-permute-start(bf16[8,64,256]{2,1,0:T(8,128)(2,1)S(1)} %get-tuple-element.28), channel_id=1, source_target_pairs={{0,1},{1,0},{2,3},{3,2},{4,5},{5,4},{6,7},{7,6},{8,9},{9,8},{10,11... | collective-permute-start | bytes 786440 | tf_op jit(solution)/shard_map/ppermute | solution.py:382

commit v3 on v2

--- a/solution.py
+++ b/solution.py
@@ -14,6 +14,7 @@
 MMAX = 24
 LANES = 128
 SPLITS = 3
+EARLY = 2
 
 SIN_POLY = (4.442882919124345, -7.308245686509103, 3.6063542184332804, -0.8461116503752865, 0.10982451642699691)
 COS_POLY = (1.4142134962552289, -6.978850948563853, 5.7394603769076955, -1.8835579059892091, 0.31068802753070307)
@@ -98,33 +99,59 @@
             o_ref[s] = nt_dot(pick, kind_rows).astype(jnp.bfloat16)
 
 
-def main_kernel(
-    ra_ref, rb_ref, xc_ref, xr_ref, oc_ref, or_ref, rad_ref, b_hbm, own_ref, oth_ref,
-    b_ref, sem, ms_ref, rads_ref, sel_ref, gca_ref, gsa_ref, cf_ref, acc_ref, proj_ref, mix_ref,
-    gcc_ref, gsc_ref,
-    *, nband, scale, qscale, chunk, group,
+def build(i, x_ref, o_ref, rads_ref, ms_ref, sel, put):
+    n = x_ref.shape[1]
+    ngroups = ms_ref.shape[2] // LANES
+    step = 16 if n % 16 == 0 else n
+    blocks = 4 if n % 64 == 0 else 1
+
+    def select(s):
+        sel[s, :n] = nn_dot(o_ref[s], rads_ref[i])
+
+    def rows(first):
+        m = [ms_ref[i, c : c + 1, :] for c in range(3)]
+        for a in range(first, first + n // blocks, step):
+            turns = 0.0
+            for c in range(3):
+                x = x_ref[c, a : a + step, :]
+                turns = turns + jnp.concatenate([x] * ngroups, axis=1) * m[c]
+            cos, sin = cos_sin_turns(turns)
+            for s in range(SHELLS):
+                v = sel[s, a : a + step, :]
+                put(s * n + a, step, (v * cos).astype(jnp.bfloat16), (v * sin).astype(jnp.bfloat16))
+
+    return [functools.partial(select, s) for s in range(SHELLS)] + [
+        functools.partial(rows, k * (n // blocks)) for k in range(blocks)
+    ]
+
+
+def mingle(first, second):
+    done = 0
+    for k, piece in enumerate(first):
+        piece()
+        upto = (k + 1) * len(second) // len(first)
+        for other in second[done:upto]:
+            other()
+        done = upto
+
+
+def unrolled(count):
+    return count <= 16
+
+
+def early_kernel(
+    ra_ref, xc_ref, xr_ref, oc_ref, or_ref, rad_ref,
+    ms_ref, rads_ref, gca_ref, gsa_ref, gcc_ref, gsc_ref, sel_ref,
+    *, nband, half, scale, qscale
 ):
-    nga = ms_ref.shape[0]
-    npw = ms_ref.shape[2]
+    nga, _, npw = ms_ref.shape
     ngroups = npw // LANES
-    half = own_ref.shape[1] // nband
-    nb = 2 * own_ref.shape[1]
-    nc = xc_ref.shape[1]
-    nr = xr_ref.shape[1]
-    nrows = b_ref.shape[0]
     qbins = rad_ref.shape[1]
     per = rads_ref.shape[1] // SPLITS
-    nsteps = nga // group
-
-    copies = [
-        pltpu.make_async_copy(b_hbm.at[pl.ds(k * chunk, chunk)], b_ref.at[pl.ds(k * chunk, chunk)], sem.at[k])
-        for k in range(nrows // chunk)
-    ]
-    for copy in copies:
-        copy.start()
+    first = half * ngroups
 
     def prepare(i):
-        raw = ra_ref[i * nband, half * ngroups :, :].astype(jnp.float32)
+        raw = ra_ref[i * nband, first:, :].astype(jnp.float32)
         comps = [
             jnp.concatenate([raw[c * ngroups + g : c * ngroups + g + 1] for g in range(ngroups)], axis=1)
             for c in range(3)
@@ -141,21 +168,62 @@
         r = (r[0:per] + r[per : 2 * per] + r[2 * per : 3 * per]) * jnp.float32(scale)
         rads_ref[i] = jnp.concatenate(split3(r), axis=0)
 
-    def build(i, x_ref, o_ref, n, sel, put):
-        rads = rads_ref[i]
-        for s in range(SHELLS):
-            sel[s, :n] = nn_dot(o_ref[s], rads)
-        m = [ms_ref[i, c : c + 1, :] for c in range(3)]
-        step = 16 if n % 16 == 0 else n
-        for a in range(0, n, step):
-            turns = 0.0
-            for c in range(3):
-                x = x_ref[c, a : a + step, :]
-                turns = turns + jnp.concatenate([x] * ngroups, axis=1) * m[c]
-            cos, sin = cos_sin_turns(turns)
-            for s in range(SHELLS):
-                v = sel[s, a : a + step, :]
-                put(s * n + a, step, (v * cos).astype(jnp.bfloat16), (v * sin).astype(jnp.bfloat16))
+    if unrolled(nga):
+        for i in range(nga):
+            prepare(i)
+    else:
+        def body(i, carry):
+            prepare(i)
+            return carry
+
+        lax.fori_loop(0, nga, body, 0)
+
+    def rebuild(i, slot):
+        def put(row, count, c, s):
+            gcc_ref[i, row : row + count, :] = c
+            gsc_ref[i, row : row + count, :] = s
+
+        return build(i, xr_ref, or_ref, rads_ref, ms_ref, sel_ref.at[slot], put)
+
+    def start(i, slot):
+        lanes = slice(i * npw, (i + 1) * npw)
+
+        def put(row, count, c, s):
+            gca_ref[row : row + count, lanes] = c
+            gsa_ref[row : row + count, lanes] = s
+
+        return build(i, xc_ref, oc_ref, rads_ref, ms_ref, sel_ref.at[slot], put)
+
+    for i in range(gca_ref.shape[1] // npw):
+        mingle(start(i, i % 2), [])
+    for i in range(gcc_ref.shape[0]):
+        mingle(rebuild(i, i % 2), [])
+
+
+def main_kernel(
+    ra_ref, rb_ref, xc_ref, xr_ref, oc_ref, or_ref, ms_ref, rads_ref, gc0_ref, gs0_ref,
+    gce_ref, gse_ref, b_hbm,
+    own_ref, oth_ref, b_ref, sem, sel_ref, gca_ref, gsa_ref, cf_ref, acc_ref, proj_ref, mix_ref,
+    gcc_ref, gsc_ref,
+    *, nband, chunk, group,
+):
+    nga = ms_ref.shape[0]
+    npw = ms_ref.shape[2]
+    ngroups = npw // LANES
+    half = own_ref.shape[1] // nband
+    nb = 2 * own_ref.shape[1]
+    nc = xc_ref.shape[1]
+    nr = xr_ref.shape[1]
+    nrows = b_ref.shape[0]
+    early = gce_ref.shape[0] if unrolled(nga) else 0
+    nsteps = nga // group
+
+    copies = [
+        pltpu.make_async_copy(b_hbm.at[pl.ds(k * chunk, chunk)], b_ref.at[pl.ds(k * chunk, chunk)], sem.at[k])
+        for k in range(nrows // chunk)
+    ]
+    for copy in copies:
+        copy.start()
 
     def weights(i):
         return [ms_ref[i, c : c + 1, :] * jnp.float32(1.0 / MMAX) for c in range(3)]
@@ -171,7 +239,8 @@
                 )
         return jnp.concatenate(rows, axis=0)
 
-    def stage(step, slot):
+    def stage(step, slot, ready=False):
+        pieces = []
         for e in range(group):
             i = step * group + e
             lanes = slice(e * npw, (e + 1) * npw)
@@ -180,48 +249,55 @@
                 gca_ref[slot, row : row + count, lanes] = c
                 gsa_ref[slot, row : row + count, lanes] = s
 
-            prepare(i)
-            build(i, xc_ref, oc_ref, nc, sel_ref.at[slot], put)
-            c = coefs(i)
-            cf = c.astype(jnp.float32)
-            w = weights(i)
-            cf_ref[slot, :nb, lanes] = c
-            for k in range(3):
-                cf_ref[slot, (k + 1) * nb : (k + 2) * nb, lanes] = (cf * w[k]).astype(jnp.bfloat16)
-
-    def consume(slot):
-        acc_ref[:, :nb] += nt_dot(gca_ref[slot], cf_ref[slot, :nb])
-        acc_ref[:, nb:] += nt_dot(gsa_ref[slot], cf_ref[slot, nb:])
+            def scaled(i=i, lanes=lanes):
+                c = coefs(i)
+                cf = c.astype(jnp.float32)
+                w = weights(i)
+                cf_ref[slot, :nb, lanes] = c
+                for k in range(3):
+                    cf_ref[slot, (k + 1) * nb : (k + 2) * nb, lanes] = (cf * w[k]).astype(jnp.bfloat16)
+
+            if not ready:
+                pieces.extend(build(i, xc_ref, oc_ref, rads_ref, ms_ref, sel_ref.at[slot], put))
+            pieces.append(scaled)
+        return pieces
+
+    def consume(gc, gs, slot):
+        def cosines(s):
+            rows = slice(s * nc, (s + 1) * nc)
+            acc_ref[rows, :nb] += nt_dot(gc[rows, :], cf_ref[slot, :nb])
+
+        def sines(s):
+            rows = slice(s * nc, (s + 1) * nc)
+            acc_ref[rows, nb:] += nt_dot(gs[rows, :], cf_ref[slot, nb:])
+
+        return [functools.partial(f, s) for s in range(SHELLS) for f in (cosines, sines)]
+
+    def consume_slot(slot):
+        return consume(gca_ref.at[slot], gsa_ref.at[slot], slot)
 
     def clear(k, carry):
         acc_ref[pl.ds(pl.multiple_of(k * nc, 8), nc), :] = jnp.zeros((nc, acc_ref.shape[1]), jnp.float32)
         return carry
 
     lax.fori_loop(0, SHELLS, clear, 0)
-    stage(0, 0)
+    mingle(stage(0, 0, ready=True), [])
+    last = consume(gc0_ref, gs0_ref, 0)
     if nsteps <= 8:
         for step in range(1, nsteps):
-            stage(step, step % 2)
-            consume((step - 1) % 2)
+            mingle(stage(step, step % 2), last)
+            last = consume_slot(step % 2)
     else:
+        mingle(stage(1, 1), last)
+
         def body(step, carry):
             slot = step % 2
-            stage(step, slot)
-            consume(1 - slot)
+            mingle(stage(step, slot), consume_slot(1 - slot))
             return carry
 
-        lax.fori_loop(1, nsteps, body, 0)
-    def rebuild(i, slot):
-        def put(row, count, c, s):
-            gcc_ref[i, row : row + count, :] = c
-            gsc_ref[i, row : row + count, :] = s
-
-        build(i, xr_ref, or_ref, nr, sel_ref.at[slot], put)
-
-    early = 4 if nga <= 16 else 0
-    for i in range(early):
-        rebuild(i, i % 2)
-    consume((nsteps - 1) % 2)
+        lax.fori_loop(2, nsteps, body, 0)
+        last = consume_slot((nsteps - 1) % 2)
+    mingle([lambda: None], last)
 
     for s in range(SHELLS):
         for t in range(COMPS):
@@ -230,23 +306,30 @@
             ]
     proj = proj_ref[...].astype(jnp.bfloat16)
 
+    def rebuild(i, slot):
+        def put(row, count, c, s):
+            gcc_ref[i - early, row : row + count, :] = c
+            gsc_ref[i - early, row : row + count, :] = s
+
+        return build(i, xr_ref, or_ref, rads_ref, ms_ref, sel_ref.at[slot], put)
+
     def multiply(first, count):
         mix_ref[first : first + count, :] = nn_dot(b_ref[first : first + count, :], proj)
 
     for copy in copies:
         copy.wait()
     nmul = nrows // chunk
-    if nga <= 16:
+    if unrolled(nga):
         for k in range(nmul):
             multiply(k * chunk, chunk)
             for i in range(early + k * (nga - early) // nmul, early + (k + 1) * (nga - early) // nmul):
-                rebuild(i, i % 2)
+                mingle(rebuild(i, i % 2), [])
     else:
         for k in range(nmul):
             multiply(k * chunk, chunk)
 
         def again(i, carry):
-            rebuild(i, i % 2)
+            mingle(rebuild(i, i % 2), [])
             return carry
 
         lax.fori_loop(0, nga, again, 0)
@@ -261,15 +344,16 @@
     mt = jnp.concatenate(mixed[1:], axis=0).astype(jnp.bfloat16)
 
     def expand(i):
-        y = nn_dot(m0, gcc_ref[i])
-        ys = nn_dot(mt, gsc_ref[i])
+        here = unrolled(nga) and i < early
+        y = nn_dot(m0, gce_ref[i] if here else gcc_ref[i - early])
+        ys = nn_dot(mt, gse_ref[i] if here else gsc_ref[i - early])
         w = weights(i)
         for k in range(3):
             y = y + w[k] * ys[k * nb : (k + 1) * nb]
         own_ref[i] = y[: nb // 2]
         oth_ref[i] = y[nb // 2 :].astype(jnp.bfloat16)
 
-    if nga <= 16:
+    if unrolled(nga):
         for i in range(nga):
             expand(i)
     else:
@@ -349,12 +433,28 @@
     vmem = pl.BlockSpec(memory_space=pltpu.VMEM)
     nmax = max(nc, nr)
     group = 2 if nga % 2 == 0 else 1
+    early = min(EARLY, nga // 2)
+    kept = nga - early if unrolled(nga) else nga
+    ms, rads, gc0, gs0, gce, gse = pl.pallas_call(
+        functools.partial(
+            early_kernel, nband=nband, half=half, scale=scale, qscale=(qbins - 1) / (3.0 * MMAX * MMAX)
+        ),
+        out_shape=[
+            jax.ShapeDtypeStruct((nga, 8, npw), jnp.float32),
+            jax.ShapeDtypeStruct((nga, width, npw), jnp.bfloat16),
+            jax.ShapeDtypeStruct((SHELLS * nc, group * npw), jnp.bfloat16),
+            jax.ShapeDtypeStruct((SHELLS * nc, group * npw), jnp.bfloat16),
+            jax.ShapeDtypeStruct((early, SHELLS * nr, npw), jnp.bfloat16),
+            jax.ShapeDtypeStruct((early, SHELLS * nr, npw), jnp.bfloat16),
+        ],
+        scratch_shapes=[pltpu.VMEM((2, SHELLS, nmax, npw), jnp.float32)],
+        compiler_params=pltpu.CompilerParams(vmem_limit_bytes=32 * 1024 * 1024),
+        cost_estimate=pl.CostEstimate(flops=10**9, transcendentals=0, bytes_accessed=10**6),
+        name="early",
+    )(ra, xc, xr, oc, orr, table)
     own, other = pl.pallas_call(
-        functools.partial(
-            main_kernel, nband=nband, scale=scale, qscale=(qbins - 1) / (3.0 * MMAX * MMAX), chunk=chunk,
-            group=group,
-        ),
-        in_specs=[vmem] * 7 + [pl.BlockSpec(memory_space=pl.ANY)],
+        functools.partial(main_kernel, nband=nband, chunk=chunk, group=group),
+        in_specs=[vmem] * 12 + [pl.BlockSpec(memory_space=pl.ANY)],
         out_specs=[vmem, vmem],
         out_shape=[
             jax.ShapeDtypeStruct((nga, nb // 2, npw), jnp.float32),
@@ -363,8 +463,6 @@
         scratch_shapes=[
             pltpu.VMEM((nrows, ncols), jnp.bfloat16),
             pltpu.SemaphoreType.DMA((nrows // chunk,)),
-            pltpu.VMEM((nga, 8, npw), jnp.float32),
-            pltpu.VMEM((nga, width, npw), jnp.bfloat16),
             pltpu.VMEM((2, SHELLS, nmax, npw), jnp.float32),
             pltpu.VMEM((2, SHELLS * nc, group * npw), jnp.bfloat16),
             pltpu.VMEM((2, SHELLS * nc, group * npw), jnp.bfloat16),
@@ -372,12 +470,12 @@
             pltpu.VMEM((SHELLS * nc, COMPS * nb), jnp.float32),
             pltpu.VMEM((ncols, nb), jnp.float32),
             pltpu.VMEM((nrows, nb), jnp.float32),
-            pltpu.VMEM((nga, SHELLS * nr, npw), jnp.bfloat16),
-            pltpu.VMEM((nga, SHELLS * nr, npw), jnp.bfloat16),
+            pltpu.VMEM((kept, SHELLS * nr, npw), jnp.bfloat16),
+            pltpu.VMEM((kept, SHELLS * nr, npw), jnp.bfloat16),
         ],
-        compiler_params=pltpu.CompilerParams(vmem_limit_bytes=50 * 1024 * 1024),
+        compiler_params=pltpu.CompilerParams(vmem_limit_bytes=46 * 1024 * 1024),
         name="apply",
-    )(ra, rb, xc, xr, oc, orr, table, coupling)
+    )(ra, rb, xc, xr, oc, orr, ms, rads, gc0, gs0, gce, gse, coupling)
 
     theirs = lax.ppermute(other, "band", pair)
     pairs = (own + theirs.astype(jnp.float32)).astype(jnp.bfloat16).reshape(ndev, half, npw)

time: 49 us -> 47.1 us (0.961)
  waiting for transfers between devices: 9.63 us -> 8.06 us
  Pallas kernels: 14.5 us -> 13.9 us
    ppermute x1, waiting for transfers between devices: 1.63 us -> 0.22 us  [shards(): rb = lax.ppermute(ra, 'band', pair)]
    pallas_call x1 -> x2, Pallas kernels: 10.8 us -> 10.2 us  [the longest x1 8.83 us: shards(): pl.pallas_call(functools.partial(main_kernel, nband=nband, chunk=chunk, g...]
  transfers between devices with their start and end apart: 3 -> 3, of which waited for: 3 -> 3; matrix products, arithmetic and copies ran while one was open for 5% -> 5% of each run, Pallas kernels for 3% -> 6%
where the time goes in v3:
time: 47.1 us; the launch traced here: 46.4 us
  Pallas kernels  13.9 us (30%)
  blocking collectives  12.7 us (27%)
  waiting for transfers between devices  8.06 us (17%)
  starting transfers between devices  7.7 us (16%)
  local copies, waits for them, and re-layouts  3.85 us (8%)
    all_to_all x1, blocking collectives, shards(): back = lax.all_to_all(pairs, axes, 0, 0).reshape(ndev // 2, 2, half, npw)  12.7 us
    pallas_call x1, Pallas kernels, shards(): pl.pallas_call(functools.partial(main_kernel, nband=nband, chunk=chunk, g...  8.83 us
    all_to_all x1, starting transfers between devices, shards(): ra = lax.all_to_all(sent, axes, 0, 0)  7.33 us
    all_to_all x1, waiting for transfers between devices, shards(): ra = lax.all_to_all(sent, axes, 0, 0)  6.61 us
    pallas_call x1, Pallas kernels, shards(): pl.pallas_call(functools.partial(table_kernel, kinds=kinds), out_shape=[j...  1.51 us
    pallas_call x1, Pallas kernels, pack(): pl.pallas_call(pack_kernel, out_shape=jax.ShapeDtypeStruct((ndev // 2, 2,...  1.49 us
    unnamed x6, local copies, waits for them, and re-layouts  1.4 us
    pallas_call x1, Pallas kernels, shards(): pl.pallas_call(functools.partial(early_kernel, nband=nband, half=half, sc...  1.39 us
  transfers between devices with their start and end apart: 3, of which 3 were waited for; matrix products, arithmetic and copies ran while one was open for 5% of the time, Pallas kernels for 6%

profile of v3, /device:TPU:0, one launch (start us, length us, event | category | flops | bytes accessed | tf_op | source)
XLA Modules:
  0.0 46.4 jit_solution(13112690345016038222)
XLA Ops:
  0.0 1.5 %pack.1 = bf16[16,2,40,128]{3,2,1,0:T(8,128)(2,1)} custom-call(bf16[32,256]{1,0:T(8,128)(2,1)} %bitcast.11, s32[3,256]{1,0:T(4,128)} %mil_ref.1), custom_call_target="tpu_custom_call" | custom-call | tf_op jit(solution)/shard_map/pack/pallas_call | solution.py:76
  1.5 7.3 %all-to-all-start = ((bf16[32,40,128]{2,1,0:T(8,128)(2,1)}), bf16[32,40,128]{2,1,0:T(8,128)(2,1)S(1)}, u32[]{:S(2)}, u32[]{:S(2)}) async-start(bf16[32,40,128]{2,1,0:T(8,128)(2,1)} %bitcast.15), calls=%async_computation | async-start | bytes 655360 | tf_op jit(solution)/shard_map/all_to_all | solution.py:403
  8.8 0.7 %reshape.25 = f32[4,3,128]{2,1,0:T(4,128)S(1)} reshape(f32[12,128]{1,0:T(8,128)} %param.13) | data formatting | bytes 12288 | tf_op jit(solution)/shard_map/reshape | solution.py:409
  9.6 0.8 %dynamic_slice.7 = s32[1536]{0:T(1024)S(1)} dynamic-slice(s32[12288]{0:T(1024)} %param.11, s32[]{:T(128)S(6)} %select_n.7), dynamic_slice_sizes={1536} | dynamic-slice | bytes 12292 | tf_op jit(solution)/shard_map/dynamic_slice | solution.py:407
  10.3 0.7 %dynamic_slice.6 = s32[3072]{0:T(1024)S(1)} dynamic-slice(s32[12288]{0:T(1024)} %param.11, s32[]{:T(128)S(6)} %select_n.6), dynamic_slice_sizes={3072} | dynamic-slice | bytes 24580 | tf_op jit(solution)/shard_map/dynamic_slice | solution.py:406
  11.0 0.1 reshape.28
  11.2 0.1 reshape.27
  11.3 0.0 copy-start.1
  11.3 0.7 %copy-done.1 = f32[3,1024]{1,0:T(4,128)S(1)} copy-done((f32[3,1024]{1,0:T(4,128)S(1)}, f32[3,1024]{1,0:T(4,128)}, u32[]{:S(2)}) %copy-start.1) | copy-done | bytes 12312
  12.0 0.0 copy-start.2
  12.0 0.7 %copy-done.2 = s32[1024]{0:T(1024)S(1)} copy-done((s32[1024]{0:T(1024)S(1)}, s32[1024]{0:T(1024)}, u32[]{:S(2)}) %copy-start.2) | copy-done | bytes 4120
  12.7 1.5 %tables.1 = (f32[3,256,128]{2,1,0:T(8,128)S(1)}, f32[3,128,128]{2,1,0:T(8,128)S(1)}, bf16[3,256,48]{2,1,0:T(8,128)(2,1)S(1)}, bf16[3,128,48]{2,1,0:T(8,128)(2,1)S(1)}) custom-call(s32[256,1]{1,0:T(8,128)S(1)} %bitcast.10, s32[128,1]{1,0:T(8,128)S(1)} %bitcast.13, s32[1,1024]{1,0:T(1,128)S(1)} %bitcast.14, f32[3,1024]{1,0:T(4,128)S(1)} %copy-done.1), custom_call_target="tpu_custom_call" | custom-call | flops 1000000000 | bytes 1000000 | tf_op jit(solution)/shard_map/tables/pallas_call | solution.py:416
  14.3 6.6 %all-to-all-done.ra_ref = bf16[32,40,128]{2,1,0:T(8,128)(2,1)S(1)} async-done(((bf16[32,40,128]{2,1,0:T(8,128)(2,1)}), bf16[32,40,128]{2,1,0:T(8,128)(2,1)S(1)}, u32[]{:S(2)}, u32[]{:S(2)}) %all-to-all-start) | async-done | bytes 327712 | tf_op jit(solution)/shard_map/all_to_all | solution.py:403
  20.9 0.0 copy-start
  20.9 0.0 collective-permute-start
  20.9 1.4 %early.1 = (f32[8,8,256]{2,1,0:T(8,128)S(1)}, bf16[8,48,256]{2,1,0:T(8,128)(2,1)S(1)}, bf16[768,512]{1,0:T(8,128)(2,1)S(1)}, bf16[768,512]{1,0:T(8,128)(2,1)S(1)...) custom-call(bf16[32,40,128]{2,1,0:T(8,128)(2,1)S(1)} %all-to-all-done.ra_ref, ...), custom_call_target="tpu_custom_call" | custom-call | flops 1000000000 | bytes 1000000 | tf_op jit(solution)/shard_map/early/pallas_call | solution.py:438
  22.3 0.2 collective-permute-done.rb_ref
  22.5 8.8 %apply.1 = (f32[8,64,256]{2,1,0:T(8,128)S(1)}, bf16[8,64,256]{2,1,0:T(8,128)(2,1)S(1)}) custom-call(bf16[32,40,128]{2,1,0:T(8,128)(2,1)S(1)} %all-to-all-done.ra_ref, bf16[32,40,128]{2,1,0:T(8,128)(2,1)S(1)} %collective-permute-done.rb_ref, f32[3,256,128]{2,1,0:T(8,128)S(1)} %get-tuple-element.28.xc_ref, f32[3,128,128]{2,1,0:T(8,128)S(1)} %get-tuple-element.29.xr_ref, ...), custom_call_target="tpu_custom_call" | custom-call | tf_op jit(solution)/shard_map/apply/pallas_call | solution.py:455
  31.3 0.4 collective-permute-start.1
  31.7 1.2 %collective-permute-done.1 = bf16[8,64,256]{2,1,0:T(8,128)(2,1)S(1)} collective-permute-done((bf16[8,64,256]{2,1,0:T(8,128)(2,1)S(1)}, bf16[8,64,256]{2,1,0:T(8,128)(2,1)S(1)}, u32[]{:S(2)}, u32[]{:S(2)}) %collective-permute-start.1) | collective-permute-done | bytes 262176 | tf_op jit(solution)/shard_map/ppermute | solution.py:480
  32.9 0.1 add_convert_fusion
  33.0 12.7 %all_to_all.10 = bf16[32,16,256]{2,1,0:T(8,128)(2,1)S(1)} all-to-all(bf16[32,16,256]{2,1,0:T(8,128)(2,1)S(1)} %bitcast.16), channel_id=1, replica_groups=mesh['ga'=8,'band'=4] {'ga','band'}, dimensions={0} | all-to-all | bytes 524288 | tf_op jit(solution)/shard_map/all_to_all | solution.py:482
  45.7 0.0 copy-done
  45.7 0.7 %finish.1 = bf16[32,256]{1,0:T(8,128)(2,1)} custom-call(bf16[16,2,16,256]{3,2,1,0:T(8,128)(2,1)S(1)} %bitcast.9, bf16[32,256]{1,0:T(8,128)(2,1)S(1)} %bitcast.12), custom_call_target="tpu_custom_call" | custom-call | tf_op jit(solution)/shard_map/finish/pallas_call | solution.py:483
  (4 shorter events, 0.0 us)
Async XLA Ops:
  1.5 19.4 %all-to-all-start = ((bf16[32,40,128]{2,1,0:T(8,128)(2,1)}), bf16[32,40,128]{2,1,0:T(8,128)(2,1)S(1)}, u32[]{:S(2)}, u32[]{:S(2)}) async-start(bf16[32,40,128]{2,1,0:T(8,128)(2,1)} %bitcast.15), calls=%async_computation | async-start | bytes 655360 | tf_op jit(solution)/shard_map/all_to_all | solution.py:403
  11.3 0.7 %copy-start.1 = (f32[3,1024]{1,0:T(4,128)S(1)}, f32[3,1024]{1,0:T(4,128)}, u32[]{:S(2)}) copy-start(f32[3,1024]{1,0:T(4,128)} %pos_ref.1) | copy-start | bytes 36868
  12.0 0.7 %copy-start.2 = (s32[1024]{0:T(1024)S(1)}, s32[1024]{0:T(1024)}, u32[]{:S(2)}) copy-start(s32[1024]{0:T(1024)} %param.10) | copy-start | bytes 12292
  20.9 24.9 %copy-start = (bf16[256,32]{0,1:T(8,128)(2,1)S(1)}, bf16[256,32]{0,1:T(8,128)(2,1)}, u32[]{:S(2)}) copy-start(bf16[256,32]{0,1:T(8,128)(2,1)} %param.7) | copy-start | bytes 49156
  20.9 1.6 %collective-permute-start = (bf16[32,40,128]{2,1,0:T(8,128)(2,1)S(1)}, bf16[32,40,128]{2,1,0:T(8,128)(2,1)S(1)}, u32[]{:S(2)}, u32[]{:S(2)}) collective-permute-start(bf16[32,40,128]{2,1,0:T(8,128)(2,1)S(1)} %all-to-all-done.ra_ref), channel_id=1, source_target_pairs={{0,1},{1,0},{2,3},{3,2},{4,5},{5,4},{6,7},{7,6},{8,9},{9,8},{10,11... | collective-permute-start | bytes 983048 | tf_op jit(solution)/shard_map/ppermute | solution.py:430
  31.3 1.6 %collective-permute-start.1 = (bf16[8,64,256]{2,1,0:T(8,128)(2,1)S(1)}, bf16[8,64,256]{2,1,0:T(8,128)(2,1)S(1)}, u32[]{:S(2)}, u32[]{:S(2)}) collective-permute-start(bf16[8,64,256]{2,1,0:T(8,128)(2,1)S(1)} %get-tuple-element.40), channel_id=1, source_target_pairs={{0,1},{1,0},{2,3},{3,2},{4,5},{5,4},{6,7},{7,6},{8,9},{9,8},{10,11... | collective-permute-start | bytes 786440 | tf_op jit(solution)/shard_map/ppermute | solution.py:480

commit v4 on v3

--- a/solution.py
+++ b/solution.py
@@ -14,7 +14,7 @@
 MMAX = 24
 LANES = 128
 SPLITS = 3
-EARLY = 2
+EARLY = 3
 
 SIN_POLY = (4.442882919124345, -7.308245686509103, 3.6063542184332804, -0.8461116503752865, 0.10982451642699691)
 COS_POLY = (1.4142134962552289, -6.978850948563853, 5.7394603769076955, -1.8835579059892091, 0.31068802753070307)
@@ -203,15 +203,15 @@
 def main_kernel(
     ra_ref, rb_ref, xc_ref, xr_ref, oc_ref, or_ref, ms_ref, rads_ref, gc0_ref, gs0_ref,
     gce_ref, gse_ref, b_hbm,
-    own_ref, oth_ref, b_ref, sem, sel_ref, gca_ref, gsa_ref, cf_ref, acc_ref, proj_ref, mix_ref,
-    gcc_ref, gsc_ref,
+    oth_ref, mine_ref, gcc_ref, gsc_ref,
+    b_ref, sem, sel_ref, gca_ref, gsa_ref, cf_ref, acc_ref, proj_ref, mix_ref,
     *, nband, chunk, group,
 ):
     nga = ms_ref.shape[0]
     npw = ms_ref.shape[2]
     ngroups = npw // LANES
-    half = own_ref.shape[1] // nband
-    nb = 2 * own_ref.shape[1]
+    half = oth_ref.shape[1] // nband
+    nb = 2 * oth_ref.shape[1]
     nc = xc_ref.shape[1]
     nr = xr_ref.shape[1]
     nrows = b_ref.shape[0]
@@ -340,28 +340,38 @@
             [mix_ref[pl.ds(COMPS * s + t, nr, stride=NCH), :] for s in range(SHELLS)], axis=0
         )
         mixed.append(m.T)
-    m0 = mixed[0].astype(jnp.bfloat16)
-    mt = jnp.concatenate(mixed[1:], axis=0).astype(jnp.bfloat16)
-
-    def expand(i):
+    mine_ref[...] = jnp.concatenate([m[: nb // 2] for m in mixed], axis=0).astype(jnp.bfloat16)
+    theirs = jnp.concatenate([m[nb // 2 :] for m in mixed], axis=0).astype(jnp.bfloat16)
+    expand(theirs, ms_ref, gce_ref, gse_ref, gcc_ref, gsc_ref, oth_ref)
+
+
+def expand(mixed, ms_ref, gce_ref, gse_ref, gcc_ref, gsc_ref, out_ref):
+    nga = ms_ref.shape[0]
+    rows = out_ref.shape[1]
+    early = gce_ref.shape[0] if unrolled(nga) else 0
+
+    def one(i):
         here = unrolled(nga) and i < early
-        y = nn_dot(m0, gce_ref[i] if here else gcc_ref[i - early])
-        ys = nn_dot(mt, gse_ref[i] if here else gsc_ref[i - early])
-        w = weights(i)
+        y = nn_dot(mixed[:rows], gce_ref[i] if here else gcc_ref[i - early])
+        ys = nn_dot(mixed[rows:], gse_ref[i] if here else gsc_ref[i - early])
         for k in range(3):
-            y = y + w[k] * ys[k * nb : (k + 1) * nb]
-        own_ref[i] = y[: nb // 2]
-        oth_ref[i] = y[nb // 2 :].astype(jnp.bfloat16)
+            w = ms_ref[i, k : k + 1, :] * jnp.float32(1.0 / MMAX)
+            y = y + w * ys[k * rows : (k + 1) * rows]
+        out_ref[i] = y.astype(out_ref.dtype)
 
     if unrolled(nga):
         for i in range(nga):
-            expand(i)
+            one(i)
     else:
         def body(i, carry):
-            expand(i)
+            one(i)
             return carry
 
         lax.fori_loop(0, nga, body, 0)
+
+
+def own_kernel(mine_ref, ms_ref, gce_ref, gse_ref, gcc_ref, gsc_ref, own_ref):
+    expand(mine_ref[...], ms_ref, gce_ref, gse_ref, gcc_ref, gsc_ref, own_ref)
 
 
 def row_chunk(count):
@@ -452,13 +462,15 @@
         cost_estimate=pl.CostEstimate(flops=10**9, transcendentals=0, bytes_accessed=10**6),
         name="early",
     )(ra, xc, xr, oc, orr, table)
-    own, other = pl.pallas_call(
+    other, mine, gcc, gsc = pl.pallas_call(
         functools.partial(main_kernel, nband=nband, chunk=chunk, group=group),
         in_specs=[vmem] * 12 + [pl.BlockSpec(memory_space=pl.ANY)],
-        out_specs=[vmem, vmem],
+        out_specs=[vmem] * 4,
         out_shape=[
-            jax.ShapeDtypeStruct((nga, nb // 2, npw), jnp.float32),
             jax.ShapeDtypeStruct((nga, nb // 2, npw), jnp.bfloat16),
+            jax.ShapeDtypeStruct((COMPS * nb // 2, SHELLS * nr), jnp.bfloat16),
+            jax.ShapeDtypeStruct((kept, SHELLS * nr, npw), jnp.bfloat16),
+            jax.ShapeDtypeStruct((kept, SHELLS * nr, npw), jnp.bfloat16),
         ],
         scratch_shapes=[
             pltpu.VMEM((nrows, ncols), jnp.bfloat16),
@@ -470,14 +482,19 @@
             pltpu.VMEM((SHELLS * nc, COMPS * nb), jnp.float32),
             pltpu.VMEM((ncols, nb), jnp.float32),
             pltpu.VMEM((nrows, nb), jnp.float32),
-            pltpu.VMEM((kept, SHELLS * nr, npw), jnp.bfloat16),
-            pltpu.VMEM((kept, SHELLS * nr, npw), jnp.bfloat16),
         ],
         compiler_params=pltpu.CompilerParams(vmem_limit_bytes=46 * 1024 * 1024),
         name="apply",
     )(ra, rb, xc, xr, oc, orr, ms, rads, gc0, gs0, gce, gse, coupling)
 
     theirs = lax.ppermute(other, "band", pair)
+    own = pl.pallas_call(
+        own_kernel,
+        out_shape=jax.ShapeDtypeStruct((nga, nb // 2, npw), jnp.float32),
+        compiler_params=pltpu.CompilerParams(vmem_limit_bytes=32 * 1024 * 1024),
+        cost_estimate=pl.CostEstimate(flops=10**9, transcendentals=0, bytes_accessed=10**6),
+        name="own",
+    )(mine, ms, gce, gse, gcc, gsc)
     pairs = (own + theirs.astype(jnp.float32)).astype(jnp.bfloat16).reshape(ndev, half, npw)
     back = lax.all_to_all(pairs, axes, 0, 0).reshape(ndev // 2, 2, half, npw)
     return pl.pallas_call(

time: 47.1 us -> 46.8 us (level)
  waiting for transfers between devices: 8.06 us -> 7.06 us
  Pallas kernels: 13.9 us -> 14.4 us
    ppermute x1, waiting for transfers between devices: 1.23 us -> 0.35 us  [shards(): theirs = lax.ppermute(other, 'band', pair)]
    pallas_call x0 -> x1, Pallas kernels: none -> 0.8 us  [shards(): pl.pallas_call(own_kernel, out_shape=jax.ShapeDtypeStruct((nga, nb // 2,...]
  transfers between devices with their start and end apart: 3 -> 3, of which waited for: 3 -> 3; matrix products, arithmetic and copies ran while one was open for 5% -> 5% of each run, Pallas kernels for 6% -> 8%
where the time goes in v4:
time: 46.8 us; the launch traced here: 46.1 us
  Pallas kernels  14.4 us (31%)
  blocking collectives  12.7 us (27%)
  starting transfers between devices  7.86 us (17%)
  waiting for transfers between devices  7.06 us (15%)
  local copies, waits for them, and re-layouts  3.85 us (8%)
    all_to_all x1, blocking collectives, shards(): back = lax.all_to_all(pairs, axes, 0, 0).reshape(ndev // 2, 2, half, npw)  12.7 us
    pallas_call x1, Pallas kernels, shards(): pl.pallas_call(functools.partial(main_kernel, nband=nband, chunk=chunk, g...  8.45 us
    all_to_all x1, starting transfers between devices, shards(): ra = lax.all_to_all(sent, axes, 0, 0)  7.33 us
    all_to_all x1, waiting for transfers between devices, shards(): ra = lax.all_to_all(sent, axes, 0, 0)  6.61 us
    pallas_call x1, Pallas kernels, shards(): pl.pallas_call(functools.partial(early_kernel, nband=nband, half=half, sc...  1.52 us
    pallas_call x1, Pallas kernels, shards(): pl.pallas_call(functools.partial(table_kernel, kinds=kinds), out_shape=[j...  1.51 us
    pallas_call x1, Pallas kernels, pack(): pl.pallas_call(pack_kernel, out_shape=jax.ShapeDtypeStruct((ndev // 2, 2,...  1.49 us
    unnamed x6, local copies, waits for them, and re-layouts  1.4 us
  transfers between devices with their start and end apart: 3, of which 3 were waited for; matrix products, arithmetic and copies ran while one was open for 5% of the time, Pallas kernels for 8%

profile of v4, /device:TPU:0, one launch (start us, length us, event | category | flops | bytes accessed | tf_op | source)
XLA Modules:
  0.0 46.1 jit_solution(2362388959879383082)
XLA Ops:
  0.0 1.5 %pack.1 = bf16[16,2,40,128]{3,2,1,0:T(8,128)(2,1)} custom-call(bf16[32,256]{1,0:T(8,128)(2,1)} %bitcast.11, s32[3,256]{1,0:T(4,128)} %mil_ref.1), custom_call_target="tpu_custom_call" | custom-call | tf_op jit(solution)/shard_map/pack/pallas_call | solution.py:76
  1.5 7.3 %all-to-all-start = ((bf16[32,40,128]{2,1,0:T(8,128)(2,1)}), bf16[32,40,128]{2,1,0:T(8,128)(2,1)S(1)}, u32[]{:S(2)}, u32[]{:S(2)}) async-start(bf16[32,40,128]{2,1,0:T(8,128)(2,1)} %bitcast.15), calls=%async_computation | async-start | bytes 655360 | tf_op jit(solution)/shard_map/all_to_all | solution.py:413
  8.8 0.7 %reshape.25 = f32[4,3,128]{2,1,0:T(4,128)S(1)} reshape(f32[12,128]{1,0:T(8,128)} %param.13) | data formatting | bytes 12288 | tf_op jit(solution)/shard_map/reshape | solution.py:419
  9.6 0.8 %dynamic_slice.7 = s32[1536]{0:T(1024)S(1)} dynamic-slice(s32[12288]{0:T(1024)} %param.11, s32[]{:T(128)S(6)} %select_n.7), dynamic_slice_sizes={1536} | dynamic-slice | bytes 12292 | tf_op jit(solution)/shard_map/dynamic_slice | solution.py:417
  10.3 0.7 %dynamic_slice.6 = s32[3072]{0:T(1024)S(1)} dynamic-slice(s32[12288]{0:T(1024)} %param.11, s32[]{:T(128)S(6)} %select_n.6), dynamic_slice_sizes={3072} | dynamic-slice | bytes 24580 | tf_op jit(solution)/shard_map/dynamic_slice | solution.py:416
  11.0 0.1 reshape.28
  11.2 0.1 reshape.27
  11.3 0.0 copy-start.1
  11.3 0.7 %copy-done.1 = f32[3,1024]{1,0:T(4,128)S(1)} copy-done((f32[3,1024]{1,0:T(4,128)S(1)}, f32[3,1024]{1,0:T(4,128)}, u32[]{:S(2)}) %copy-start.1) | copy-done | bytes 12312
  12.0 0.0 copy-start.2
  12.0 0.7 %copy-done.2 = s32[1024]{0:T(1024)S(1)} copy-done((s32[1024]{0:T(1024)S(1)}, s32[1024]{0:T(1024)}, u32[]{:S(2)}) %copy-start.2) | copy-done | bytes 4120
  12.7 1.5 %tables.1 = (f32[3,256,128]{2,1,0:T(8,128)S(1)}, f32[3,128,128]{2,1,0:T(8,128)S(1)}, bf16[3,256,48]{2,1,0:T(8,128)(2,1)S(1)}, bf16[3,128,48]{2,1,0:T(8,128)(2,1)S(1)}) custom-call(s32[256,1]{1,0:T(8,128)S(1)} %bitcast.10, s32[128,1]{1,0:T(8,128)S(1)} %bitcast.13, s32[1,1024]{1,0:T(1,128)S(1)} %bitcast.14, f32[3,1024]{1,0:T(4,128)S(1)} %copy-done.1), custom_call_target="tpu_custom_call" | custom-call | flops 1000000000 | bytes 1000000 | tf_op jit(solution)/shard_map/tables/pallas_call | solution.py:426
  14.3 6.6 %all-to-all-done.ra_ref = bf16[32,40,128]{2,1,0:T(8,128)(2,1)S(1)} async-done(((bf16[32,40,128]{2,1,0:T(8,128)(2,1)}), bf16[32,40,128]{2,1,0:T(8,128)(2,1)S(1)}, u32[]{:S(2)}, u32[]{:S(2)}) %all-to-all-start) | async-done | bytes 327712 | tf_op jit(solution)/shard_map/all_to_all | solution.py:413
  20.9 0.0 collective-permute-start
  20.9 1.5 %early.1 = (f32[8,8,256]{2,1,0:T(8,128)S(1)}, bf16[8,48,256]{2,1,0:T(8,128)(2,1)S(1)}, bf16[768,512]{1,0:T(8,128)(2,1)S(1)}, bf16[768,512]{1,0:T(8,128)(2,1)S(1)...) custom-call(bf16[32,40,128]{2,1,0:T(8,128)(2,1)S(1)} %all-to-all-done.ra_ref, ...), custom_call_target="tpu_custom_call" | custom-call | flops 1000000000 | bytes 1000000 | tf_op jit(solution)/shard_map/early/pallas_call | solution.py:448
  22.4 0.1 collective-permute-done.rb_ref
  22.5 0.0 copy-start
  22.5 8.4 %apply.1 = (bf16[8,64,256]{2,1,0:T(8,128)(2,1)S(1)}, bf16[256,384]{1,0:T(8,128)(2,1)S(1)}, bf16[5,384,256]{2,1,0:T(8,128)(2,1)S(1)}, bf16[5,384,256]{2,1,0:T(8,128)(2,1)S(1)}) custom-call(bf16[32,40,128]{2,1,0:T(8,128)(2,1)S(1)} %all-to-all-done.ra_ref, bf16[32,40,128]{2,1,0:T(8,128)(2,1)S(1)} %collective-permute-done.rb_ref, ...), custom_call_target="tpu_custom_call" | custom-call | tf_op jit(solution)/shard_map/apply/pallas_call | solution.py:465
  31.0 0.5 %collective-permute-start.1 = (bf16[8,64,256]{2,1,0:T(8,128)(2,1)S(1)}, bf16[8,64,256]{2,1,0:T(8,128)(2,1)S(1)}, u32[]{:S(2)}, u32[]{:S(2)}) collective-permute-start(bf16[8,64,256]{2,1,0:T(8,128)(2,1)S(1)} %get-tuple-element.44), channel_id=1, source_target_pairs={{0,1},{1,0},{2,3},{3,2},{4,5},{5,4},{6,7},{7,6},{8,9},{9,8},{10,11... | collective-permute-start | bytes 786440 | tf_op jit(solution)/shard_map/ppermute | solution.py:490
  31.5 0.8 %own.1 = f32[8,64,256]{2,1,0:T(8,128)S(1)} custom-call(bf16[256,384]{1,0:T(8,128)(2,1)S(1)} %get-tuple-element.41.mine_ref, f32[8,8,256]{2,1,0:T(8,128)S(1)} %get-tuple-element.35.ms_ref, bf16[3,384,256]{2,1,0:T(8,128)(2,1)S(1)} %get-tuple-element.39.gce_ref, bf16[3,384,256]{2,1,0:T(8,128)(2,1)S(1)} %get-tuple-element.40.gse_ref, ...), custom_call_target="tpu_custom_call" | custom-call | flops 1000000000 | bytes 1000000 | tf_op jit(solution)/shard_map/own/pallas_call | solution.py:491
  32.3 0.4 collective-permute-done.1
  32.7 0.1 add_convert_fusion
  32.7 12.7 %all_to_all.10 = bf16[32,16,256]{2,1,0:T(8,128)(2,1)S(1)} all-to-all(bf16[32,16,256]{2,1,0:T(8,128)(2,1)S(1)} %bitcast.16), channel_id=1, replica_groups=mesh['ga'=8,'band'=4] {'ga','band'}, dimensions={0} | all-to-all | bytes 524288 | tf_op jit(solution)/shard_map/all_to_all | solution.py:499
  45.4 0.0 copy-done
  45.4 0.7 %finish.1 = bf16[32,256]{1,0:T(8,128)(2,1)} custom-call(bf16[16,2,16,256]{3,2,1,0:T(8,128)(2,1)S(1)} %bitcast.9, bf16[32,256]{1,0:T(8,128)(2,1)S(1)} %bitcast.12), custom_call_target="tpu_custom_call" | custom-call | tf_op jit(solution)/shard_map/finish/pallas_call | solution.py:500
  (4 shorter events, 0.0 us)
Async XLA Ops:
  1.5 19.4 %all-to-all-start = ((bf16[32,40,128]{2,1,0:T(8,128)(2,1)}), bf16[32,40,128]{2,1,0:T(8,128)(2,1)S(1)}, u32[]{:S(2)}, u32[]{:S(2)}) async-start(bf16[32,40,128]{2,1,0:T(8,128)(2,1)} %bitcast.15), calls=%async_computation | async-start | bytes 655360 | tf_op jit(solution)/shard_map/all_to_all | solution.py:413
  11.3 0.7 %copy-start.1 = (f32[3,1024]{1,0:T(4,128)S(1)}, f32[3,1024]{1,0:T(4,128)}, u32[]{:S(2)}) copy-start(f32[3,1024]{1,0:T(4,128)} %pos_ref.1) | copy-start | bytes 36868
  12.0 0.7 %copy-start.2 = (s32[1024]{0:T(1024)S(1)}, s32[1024]{0:T(1024)}, u32[]{:S(2)}) copy-start(s32[1024]{0:T(1024)} %param.10) | copy-start | bytes 12292
  20.9 1.6 %collective-permute-start = (bf16[32,40,128]{2,1,0:T(8,128)(2,1)S(1)}, bf16[32,40,128]{2,1,0:T(8,128)(2,1)S(1)}, u32[]{:S(2)}, u32[]{:S(2)}) collective-permute-start(bf16[32,40,128]{2,1,0:T(8,128)(2,1)S(1)} %all-to-all-done.ra_ref), channel_id=1, source_target_pairs={{0,1},{1,0},{2,3},{3,2},{4,5},{5,4},{6,7},{7,6},{8,9},{9,8},{10,11... | collective-permute-start | bytes 983048 | tf_op jit(solution)/shard_map/ppermute | solution.py:440
  22.5 22.9 %copy-start = (bf16[256,32]{0,1:T(8,128)(2,1)S(1)}, bf16[256,32]{0,1:T(8,128)(2,1)}, u32[]{:S(2)}) copy-start(bf16[256,32]{0,1:T(8,128)(2,1)} %param.7) | copy-start | bytes 49156
  31.0 1.7 %collective-permute-start.1 = (bf16[8,64,256]{2,1,0:T(8,128)(2,1)S(1)}, bf16[8,64,256]{2,1,0:T(8,128)(2,1)S(1)}, u32[]{:S(2)}, u32[]{:S(2)}) collective-permute-start(bf16[8,64,256]{2,1,0:T(8,128)(2,1)S(1)} %get-tuple-element.44), channel_id=1, source_target_pairs={{0,1},{1,0},{2,3},{3,2},{4,5},{5,4},{6,7},{7,6},{8,9},{9,8},{10,11... | collective-permute-start | bytes 786440 | tf_op jit(solution)/shard_map/ppermute | solution.py:490
